TPU v7x, 256 devices: a whole 4x4x8 slice. The times are simulated.
256 devices in a mesh: dp: 64 (over y, z, core), expert: 4 (over x).
Axes of the slice: x: 4, y: 4, z: 8, core: 2. Of those that a mesh axis runs over, the one named last changes fastest.
Arguments:
- gradients: bfloat16 [64, 1024, 128, 128], P('dp', 'expert'), may hold values from -600 to 600
- owner_table: int32 [4, 256], P('expert'), may hold values from 0 to 255, as said below
- step_count: int32 [1], replicated, may hold values from 1 to 8
- master: float32 [1024, 128, 128], P(('dp', 'expert')), may hold values from -0.078125 to 0.078125
- first_code: bfloat16 [1024, 128, 128], P(('dp', 'expert')), may hold values from -1 to 1
- first_scale: float32 [1024], P(('dp', 'expert')), may hold values from 0.1 to 1
- first_power: float32 [1024], P(('dp', 'expert')), may hold values from 1 to 3
- second_code: bfloat16 [1024, 128, 128], P(('dp', 'expert')), may hold values from 0.0099487305 to 1
- second_scale: float32 [1024], P(('dp', 'expert')), may hold values from 0.1 to 2
- second_power: float32 [1024], P(('dp', 'expert')), may hold values from 1 to 3
Outputs:
- new_master: float32 [1024, 128, 128], P(('dp', 'expert'))
- new_first_code: bfloat16 [1024, 128, 128], P(('dp', 'expert'))
- new_first_scale: float32 [1024], P(('dp', 'expert'))
- new_first_power: float32 [1024], P(('dp', 'expert'))
- new_second_code: bfloat16 [1024, 128, 128], P(('dp', 'expert'))
- new_second_scale: float32 [1024], P(('dp', 'expert'))
- new_second_power: float32 [1024], P(('dp', 'expert'))
- weight_code: bfloat16 [1024, 128, 128], P('dp')
- weight_scale: bfloat16 [1024], P('dp')
Inputs may be any that keep to these rules, and one draw needn't show every extreme that they name: `owner_table`: each row is a permutation of 0 to 255.
All inputs are finite; a program needn't handle non-finite values. Where the computation divides by a largest or mean magnitude, that divisor is 1e-20 or more.
Results may differ from a plain program's by a relative error of at most 0.009.
Values may be sent and summed in bfloat16 or wider, within the bound.
No kernel may reach another device: no remote copies, remote signals or barrier semaphores. Data moves between devices by JAX's collectives and lax.ppermute only.
A program may use at most 128 MiB of HBM per device.

v0:
```python
import jax
import jax.numpy as jnp
from jax import lax
from jax.sharding import Mesh
from jax.sharding import PartitionSpec as P

DP = ("dp_0", "dp_1", "dp_2")
DP_EXPERT = ("dp_0", "dp_1", "dp_2", "expert")


BETA_ONE = 0.9
BETA_TWO = 0.95
LEARN_RATE = 0.01
WEIGHT_DECAY = 0.1
CLIP_RMS = 0.5
LOG_SPAN = 4.0
EPSILON = 1e-06
ADAM_EPS = 1e-08


def over_axes(array, axes):
    for axis in axes:
        array = lax.psum(array, axis)
    return array


def sent_together(arrays, axis, dim, along):
    columns = [a.reshape(*a.shape[:along], -1) for a in arrays]
    both = jnp.concatenate(columns, axis=along)
    filled, at, finished = (lax.all_gather(both, axis, axis=dim, tiled=True), 0, [])
    for a, column in zip(arrays, columns):
        section = filled[..., at : at + column.shape[along]]
        finished.append(section.reshape(*section.shape[:along], *a.shape[along:]))
        at += column.shape[along]
    return tuple(finished)


def decode_moment(code, scale, power):
    values = code.astype(jnp.float32)
    magnitude = jnp.power(jnp.abs(values), 1.0 / power[:, None, None])
    return scale[:, None, None] * jnp.sign(values) * magnitude


def encode_moment(values):
    absval = jnp.abs(values)
    largest = jnp.max(absval, axis=(1, 2))
    average = jnp.mean(absval, axis=(1, 2))
    power = jnp.clip(LOG_SPAN / jnp.log(1.0 + largest / (average + EPSILON)), 1.0, 3.0)
    scale = largest + EPSILON
    scaled = absval / scale[:, None, None]
    coded = (jnp.sign(values) * jnp.power(scaled, power[:, None, None])).astype(jnp.bfloat16)
    return (coded, scale, power)


def finish(
    owned_grad,
    total_sq,
    numel,
    step_count,
    master,
    first_code,
    first_scale,
    first_power,
    second_code,
    second_scale,
    second_power,
):
    clip_factor = jnp.minimum(1.0, CLIP_RMS / jnp.sqrt(total_sq / numel + EPSILON))
    grad = owned_grad * clip_factor
    first_old = decode_moment(first_code, first_scale, first_power)
    second_old = decode_moment(second_code, second_scale, second_power)
    first = BETA_ONE * first_old + (1.0 - BETA_ONE) * grad
    second = BETA_TWO * second_old + (1.0 - BETA_TWO) * grad * grad
    tcount = step_count[0].astype(jnp.float32)
    bias_one = 1.0 - jnp.power(BETA_ONE, tcount)
    bias_two = 1.0 - jnp.power(BETA_TWO, tcount)
    update = first / bias_one / (jnp.sqrt(second / bias_two) + ADAM_EPS)
    new_master = master - LEARN_RATE * (update + WEIGHT_DECAY * master)
    first_out = encode_moment(first)
    second_out = encode_moment(second)
    weight_scale = (jnp.max(jnp.abs(new_master), axis=(1, 2)) + EPSILON).astype(jnp.bfloat16)
    weight_code = (new_master / weight_scale.astype(jnp.float32)[:, None, None]).astype(
        jnp.bfloat16
    )
    return (new_master, first_out, second_out, weight_code, weight_scale)


def replica_total(received):
    return jnp.sum(received, axis=0, dtype=jnp.float32)


def on_device(
    gradients,
    owner_table,
    step_count,
    master,
    first_code,
    first_scale,
    first_power,
    second_code,
    second_scale,
    second_power,
):
    owned_count = master.shape[0]
    tile_side = master.shape[1]
    table_row = owner_table[0]
    numel = float(owned_count * lax.axis_size(DP) * lax.axis_size("expert") * tile_side * tile_side)
    permuted = jnp.take(gradients[0], table_row, axis=0)
    by_owner = permuted.reshape((lax.axis_size(DP), owned_count, tile_side, tile_side))
    owned_grad = replica_total(
        lax.all_to_all(by_owner, DP, split_axis=0, concat_axis=0, tiled=True)
    )
    total_sq = over_axes(jnp.sum(owned_grad * owned_grad), DP_EXPERT)
    new_master, first_out, second_out, weight_code, weight_scale = finish(
        owned_grad,
        total_sq,
        numel,
        step_count,
        master,
        first_code,
        first_scale,
        first_power,
        second_code,
        second_scale,
        second_power,
    )
    gathered_code, gathered_scale = sent_together((weight_code, weight_scale), "expert", 0, 1)
    return (
        new_master,
        first_out[0],
        first_out[1],
        first_out[2],
        second_out[0],
        second_out[1],
        second_out[2],
        gathered_code,
        gathered_scale,
    )


def solution(mesh):
    split = Mesh(
        mesh.devices.reshape(4, 8, 2, mesh.shape["expert"]), ("dp_0", "dp_1", "dp_2", "expert")
    )
    return jax.shard_map(
        on_device,
        mesh=split,
        in_specs=(
            P(DP, "expert", None, None),
            P("expert", None),
            P(),
            P(DP_EXPERT, None, None),
            P(DP_EXPERT, None, None),
            P(DP_EXPERT),
            P(DP_EXPERT),
            P(DP_EXPERT, None, None),
            P(DP_EXPERT),
            P(DP_EXPERT),
        ),
        out_specs=(
            P(DP_EXPERT, None, None),
            P(DP_EXPERT, None, None),
            P(DP_EXPERT),
            P(DP_EXPERT),
            P(DP_EXPERT, None, None),
            P(DP_EXPERT),
            P(DP_EXPERT),
            P(DP, None, None),
            P(DP),
        ),
        check_vma=False,
    )
```

profile of v0, /device:TPU:1, one launch (start us, length us, event | category | flops | bytes accessed | tf_op | source)
XLA Modules:
  0.0 282.4 jit_solution(9667601501916074793)
XLA Ops:
  0.6 0.7 compare_select_fusion.1
  1.3 0.5 broadcast.152
  1.8 1.3 reduce.5
  3.2 0.1 squeeze.9
  3.3 12.0 %gather_fusion = bf16[256,128,128]{2,1,0:T(8,128)(2,1)} fusion(bf16[256,128,128]{2,1,0:T(8,128)(2,1)} %bitcast.20, s32[1024]{0:T(1024)S(1)} %pad_clamp_fusion), kind=kCustom, calls=%fused_computation | custom fusion | bytes 16778240 | tf_op jit(solution)/shard_map/jit(_take)/gather | solution.py:108
  15.3 7.4 %broadcast_select_fusion = bf16[64,4,128,128]{3,2,1,0:T(8,128)(2,1)} fusion(bf16[64,4,128,128]{3,2,1,0:T(8,128)(2,1)} %bitcast.19, pred[64,4]{1,0:T(8,128)(4,1)S(1)} %compare_and_fusion), kind=kLoop, calls=%fused_computation.2 | loop fusion | flops 4194304 | bytes 16777472 | tf_op jit(solution)/shard_map/jit(_take)/select_n | solution.py:108
  22.7 0.0 copy-start.10
  22.8 13.5 %all-to-all-start = ((bf16[64,4,128,128]{3,2,1,0:T(8,128)(2,1)}), bf16[64,4,128,128]{3,2,1,0:T(8,128)(2,1)}, u32[]{:S(2)}, u32[]{:S(2)}) async-start(bf16[64,4,128,128]{3,2,1,0:T(8,128)(2,1)} %broadcast_select_fusion), calls=%async_computation | async-start | bytes 16777216 | tf_op jit(solution)/shard_map/all_to_all | solution.py:111
  36.2 0.0 copy-start.1
  36.2 0.0 copy-start.2
  36.2 0.0 copy-start.3
  36.3 0.0 copy-start.8
  36.3 0.0 copy-start.9
  37.0 0.0 copy-done.10
  37.0 0.0 copy-done.11
  37.0 184.9 %all-to-all-done = bf16[64,4,128,128]{3,2,1,0:T(8,128)(2,1)} async-done(((bf16[64,4,128,128]{3,2,1,0:T(8,128)(2,1)}), bf16[64,4,128,128]{3,2,1,0:T(8,128)(2,1)}, u32[]{:S(2)}, u32[]{:S(2)}) %all-to-all-start) | async-done | bytes 8388640 | tf_op jit(solution)/shard_map/all_to_all | solution.py:111
  222.0 5.1 %convert_reduce_fusion = f32[4,128,128]{2,1,0:T(8,128)S(1)} fusion(bf16[64,4,128,128]{3,2,1,0:T(8,128)(2,1)} %all-to-all-done), kind=kLoop, calls=%fused_computation.1 | loop fusion | flops 8323072 | bytes 8650752 | tf_op jit(solution)/shard_map/reduce_sum | solution.py:89
  227.1 0.7 multiply_reduce_fusion
  227.8 9.2 %psum.28 = f32[]{:T(128)} all-reduce(f32[]{:T(128)} %multiply_reduce_fusion), channel_id=1, replica_groups=mesh['dp_0'=4,'dp_1'=8,'dp_2'=2,'expert'=4] {'dp_0'}, use_global_device_ids=true, to_apply=%region_2.3 | all-reduce | flops 1 | bytes 8 | tf_op jit(solution)/shard_map/psum | solution.py:23
  237.1 11.7 %psum.29 = f32[]{:T(128)} all-reduce(f32[]{:T(128)} %psum.28), channel_id=1, replica_groups=mesh['dp_0'=4,'dp_1'=8,'dp_2'=2,'expert'=4] {'dp_1'}, use_global_device_ids=true, to_apply=%region_3.4 | all-reduce | flops 1 | bytes 8 | tf_op jit(solution)/shard_map/psum | solution.py:23
  248.8 8.3 %psum.30 = f32[]{:T(128)} all-reduce(f32[]{:T(128)} %psum.29), channel_id=1, replica_groups=mesh['dp_0'=4,'dp_1'=8,'dp_2'=2,'expert'=4] {'dp_2'}, use_global_device_ids=true, to_apply=%region_4.5 | all-reduce | flops 1 | bytes 8 | tf_op jit(solution)/shard_map/psum | solution.py:23
  257.0 9.1 %psum.31 = f32[]{:T(128)} all-reduce(f32[]{:T(128)} %psum.30), channel_id=1, replica_groups=mesh['dp_0'=4,'dp_1'=8,'dp_2'=2,'expert'=4] {'expert'}, use_global_device_ids=true, to_apply=%region_5.6 | all-reduce | flops 1 | bytes 8 | tf_op jit(solution)/shard_map/psum | solution.py:23
  266.8 0.0 copy-done.1
  266.8 0.0 copy-done.2
  266.8 0.0 copy-done.3
  266.8 0.0 copy-done.8
  266.9 0.0 copy-done.9
  266.9 1.1 abs_reduce_fusion
  267.9 0.1 fusion.10
  268.1 0.1 copy.28
  268.2 0.1 copy.24
  268.3 0.1 maximum_bitcast_fusion
  268.3 10.3 %all-gather = bf16[4,4,16385]{2,1,0:T(4,128)(2,1)S(1)} all-gather(bf16[1,4,16385]{2,1,0:T(4,128)(2,1)S(1)} %maximum_bitcast_fusion), channel_id=1, replica_groups=mesh['dp_0'=4,'dp_1'=8,'dp_2'=2,'expert'=4] {'expert'}, dimensions={0}, use_global_device_ids=true | all-gather | bytes 655400 | tf_op jit(solution)/shard_map/all_gather | solution.py:30
  278.6 0.2 reshape.139
  278.9 0.6 slice_reduce_fusion
  279.5 0.1 abs_reduce_fusion.3
  279.6 0.1 abs_reduce_fusion.1
  279.8 0.9 copy.26
  280.7 0.0 copy-start.4
  280.7 0.0 copy-start.5
  280.7 0.0 copy-start.6
  280.7 0.0 copy-start.7
  280.7 1.6 multiply_convert_fusion
  282.4 0.0 copy-done
  282.4 0.0 copy-done.4
  282.4 0.0 copy-done.5
  282.4 0.0 copy-done.6
  282.4 0.0 copy-done.7
  (10 shorter events, 0.1 us)
Async XLA Ops:
  22.7 14.2 %copy-start.10 = (f32[4]{0:T(128)S(1)}, f32[4]{0:T(128)}, u32[]{:S(2)}) copy-start(f32[4]{0:T(128)} %param.19) | copy-start | bytes 52
  22.7 14.3 %copy-start.11 = (f32[4]{0:T(128)S(1)}, f32[4]{0:T(128)}, u32[]{:S(2)}) copy-start(f32[4]{0:T(128)} %param.16) | copy-start | bytes 52
  22.8 199.2 %all-to-all-start = ((bf16[64,4,128,128]{3,2,1,0:T(8,128)(2,1)}), bf16[64,4,128,128]{3,2,1,0:T(8,128)(2,1)}, u32[]{:S(2)}, u32[]{:S(2)}) async-start(bf16[64,4,128,128]{3,2,1,0:T(8,128)(2,1)} %broadcast_select_fusion), calls=%async_computation | async-start | bytes 16777216 | tf_op jit(solution)/shard_map/all_to_all | solution.py:111
  36.2 230.6 %copy-start.1 = (f32[4,128,128]{2,1,0:T(8,128)S(1)}, f32[4,128,128]{2,1,0:T(8,128)}, u32[]{:S(2)}) copy-start(f32[4,128,128]{2,1,0:T(8,128)} %param.13) | copy-start | bytes 786436
  36.2 230.6 %copy-start.2 = (bf16[4,128,128]{2,1,0:T(8,128)(2,1)S(1)}, bf16[4,128,128]{2,1,0:T(8,128)(2,1)}, u32[]{:S(2)}) copy-start(bf16[4,128,128]{2,1,0:T(8,128)(2,1)} %param.17) | copy-start | bytes 393220
  36.2 230.6 %copy-start.3 = (bf16[4,128,128]{2,1,0:T(8,128)(2,1)S(1)}, bf16[4,128,128]{2,1,0:T(8,128)(2,1)}, u32[]{:S(2)}) copy-start(bf16[4,128,128]{2,1,0:T(8,128)(2,1)} %param.14) | copy-start | bytes 393220
  36.3 230.6 %copy-start.8 = (f32[4]{0:T(128)S(1)}, f32[4]{0:T(128)}, u32[]{:S(2)}) copy-start(f32[4]{0:T(128)} %param.18) | copy-start | bytes 52
  36.3 230.6 %copy-start.9 = (f32[4]{0:T(128)S(1)}, f32[4]{0:T(128)}, u32[]{:S(2)}) copy-start(f32[4]{0:T(128)} %param.15) | copy-start | bytes 52
  267.9 14.4 %copy-start = (f32[4,128,128]{2,1,0:T(8,128)}, f32[4,128,128]{2,1,0:T(8,128)S(1)}, u32[]{:S(2)}) copy-start(f32[4,128,128]{2,1,0:T(8,128)S(1)} %get-tuple-element.14) | copy-start | bytes 786436
  280.7 1.7 copy-start.4
  280.7 1.7 copy-start.5
  280.7 1.7 copy-start.6
  280.7 1.7 copy-start.7
where the time goes:
time: 285 us; the launch traced here: 282 us
  waiting for transfers between devices  185 us (65%)
  blocking collectives  48.5 us (17%)
  other arithmetic  18.5 us (6%)
  local copies, waits for them, and re-layouts  14.7 us (5%)
  starting transfers between devices  13.5 us (5%)
    all_to_all x1, waiting for transfers between devices, on_device(): lax.all_to_all(by_owner, DP, split_axis=0, concat_axis=0, tiled=True)  185 us
    psum x4, blocking collectives, over_axes(): array = lax.psum(array, axis)  38.3 us
    all_to_all x1, starting transfers between devices, on_device(): lax.all_to_all(by_owner, DP, split_axis=0, concat_axis=0, tiled=True)  13.5 us
    gather x1, local copies, waits for them, and re-layouts, on_device(): permuted = jnp.take(gradients[0], table_row, axis=0)  12 us
    all_gather x1, blocking collectives, sent_together(): lax.all_gather(both, axis, axis=dim, tiled=True)  10.3 us
    select_n x2, other arithmetic, on_device(): permuted = jnp.take(gradients[0], table_row, axis=0)  8.12 us
  transfers between devices with their start and end apart: 1, of which 1 were waited for; matrix products, arithmetic and copies ran while one was open for 0% of the time, Pallas kernels for 0%

commit v1 on v0

v1 whole, which is shorter than its diff:
```python
import jax
import jax.numpy as jnp
from jax import lax
from jax.experimental import pallas as pl
from jax.experimental.pallas import tpu as pltpu
from jax.sharding import Mesh
from jax.sharding import PartitionSpec as P

DP = ("y", "zh", "zl", "core")
Z = ("zh", "zl")
EVERY = ("y", "zh", "zl", "core", "expert")
DP_EXPERT = EVERY

OWN = 4
BETA_ONE = 0.9
BETA_TWO = 0.95
LEARN_RATE = 0.01
WEIGHT_DECAY = 0.1
CLIP_RMS = 0.5
LOG_SPAN = 4.0
EPSILON = 1e-06
ADAM_EPS = 1e-08

VMEM = pltpu.VMEM
SMEM = pltpu.SMEM

Y_EVEN = [(i, i ^ 1) for i in range(4)]
Y_ODD = [(i, i ^ 3) for i in range(4)]
Z_EVEN = [(i, i ^ 1) for i in range(8)]
Z_ODD = [(i, (i + 1) % 8 if i % 2 else (i - 1) % 8) for i in range(8)]

STEPS = (
    (("y", Y_EVEN), (Z, Z_EVEN), ("y", Y_ODD)),
    (("y", Y_ODD), (Z, Z_ODD), ("y", Y_EVEN)),
    ((Z, Z_EVEN), ("y", Y_EVEN), ("y", Y_ODD)),
    ((Z, Z_ODD), ("y", Y_ODD), ("y", Y_EVEN)),
)


def shifted(count, by):
    return [(i, (i + by) % count) for i in range(count)]


def owner_of(k, place, y, zh, zl):
    bits = ((place >> 4) & 1, (place >> 3) & 1, (place >> 2) & 1)
    shift = place & 3
    for bit, (axis, pairs) in zip(bits, STEPS[k]):
        goes = 1 - bit
        if axis == "y":
            y = y ^ (goes * (1 if pairs is Y_EVEN else 3))
        else:
            if pairs is Z_ODD:
                zh = (zh + goes * (2 * zl - 1)) & 3
            zl = zl ^ goes
    return y, (zh + shift) & 3, zl


def pick_kernel(where, table, grads, *rest):
    outs, (held, loaded, stored) = rest[:OWN], rest[OWN:]
    y, zh, zl, core = where[0], where[1], where[2], where[3]
    count = held.shape[1]

    for k in range(OWN):

        def load(place, _, k=k):
            oy, ozh, ozl = owner_of(k, place, y, zh, zl)
            slot = ((((oy * 4 + ozh) * 2 + ozl) * 2) + core) * OWN + k
            pltpu.make_async_copy(
                grads.at[table[slot]], held.at[k, place], loaded.at[k]
            ).start()
            return 0

        lax.fori_loop(0, count, load, 0, unroll=8)
    for k in range(OWN):
        pltpu.make_async_copy(outs[k], held.at[k], loaded.at[k]).wait()
        pltpu.make_async_copy(held.at[k], outs[k], stored.at[k]).start()
    for k in range(OWN):
        pltpu.make_async_copy(held.at[k], outs[k], stored.at[k]).wait()


def pick(where, table, grads):
    tile = grads.shape[1:]
    count = grads.shape[0] // (2 * OWN)
    return pl.pallas_call(
        pick_kernel,
        out_shape=[jax.ShapeDtypeStruct((count, *tile), grads.dtype)] * OWN,
        in_specs=[
            pl.BlockSpec(memory_space=SMEM),
            pl.BlockSpec(memory_space=SMEM),
            pl.BlockSpec(memory_space=pl.ANY),
        ],
        out_specs=[pl.BlockSpec(memory_space=pl.ANY)] * OWN,
        scratch_shapes=[
            VMEM((OWN, count, *tile), grads.dtype),
            pltpu.SemaphoreType.DMA((OWN,)),
            pltpu.SemaphoreType.DMA((OWN,)),
        ],
        name="pick",
    )(where, table, grads)


def root(magnitude, power):
    return jnp.exp(jnp.log(magnitude) * power)


def decode_kernel(fs, fp, ss, sp, master, first_code, second_code, out):
    for i in range(OWN):
        out[i] = master[i]
        for base, code, scale, power in ((OWN, first_code, fs, fp), (2 * OWN, second_code, ss, sp)):
            values = code[i].astype(jnp.float32)
            old = scale[i] * root(jnp.abs(values), 1.0 / jnp.full(values.shape, power[i]))
            out[base + i] = jnp.where(values < 0, -old, old)


def decode(fs, fp, ss, sp, master, first_code, second_code):
    return pl.pallas_call(
        decode_kernel,
        out_shape=jax.ShapeDtypeStruct((3 * OWN, *master.shape[1:]), jnp.float32),
        in_specs=[pl.BlockSpec(memory_space=SMEM)] * 4 + [pl.BlockSpec(memory_space=VMEM)] * 3,
        out_specs=pl.BlockSpec(memory_space=VMEM),
        name="decode",
    )(fs, fp, ss, sp, master, first_code, second_code)


def total_kernel(*refs):
    parts, (owned, row) = refs[:-2], refs[-2:]
    squares = jnp.zeros((1, owned.shape[-1]), jnp.float32)
    for k in range(OWN):
        total = parts[k][...]
        for received in parts[OWN:]:
            total = total + received[k].astype(jnp.float32)
        owned[k] = total
        squares = squares + jnp.sum(total * total, axis=0, keepdims=True)
    row[...] = jnp.broadcast_to(squares[None], row.shape)


def total(rests, received, devices):
    tile = rests[0].shape
    return pl.pallas_call(
        total_kernel,
        out_shape=[
            jax.ShapeDtypeStruct((OWN, *tile), jnp.float32),
            jax.ShapeDtypeStruct((devices, 1, tile[-1]), jnp.float32),
        ],
        in_specs=[pl.BlockSpec(memory_space=VMEM)] * (len(rests) + len(received)),
        out_specs=[pl.BlockSpec(memory_space=VMEM)] * 2,
        name="total",
    )(*rests, *received)


def encode(values, code, scales, powers, i):
    absval = jnp.abs(values)
    largest = jnp.max(absval)
    average = jnp.sum(absval) / float(values.shape[0] * values.shape[1])
    ratio = jnp.full((8, 128), largest) / (jnp.full((8, 128), average) + EPSILON)
    power = jnp.max(jnp.clip(LOG_SPAN / jnp.log(1.0 + ratio), 1.0, 3.0))
    scale = largest + EPSILON
    scales[i] = scale
    powers[i] = power
    coded = root(absval / scale, power)
    code[i] = jnp.where(values < 0, -coded, coded).astype(code.dtype)


def finish_kernel(
    numel, where, step, squares, *refs
):
    grads, states = refs[:4], refs[4:8]
    (new_master, fcode, fscale, fpower, scode, sscale, spower, wcode, wscale) = refs[8:]
    total_sq = jnp.sum(jnp.sum(squares[...], axis=0))
    mean_sq = jnp.full((8, 128), total_sq / numel + EPSILON)
    clip = jnp.max(jnp.minimum(1.0, CLIP_RMS / jnp.sqrt(mean_sq)))
    steps = jnp.full((8, 128), step[0]).astype(jnp.float32)
    bias_one = jnp.max(1.0 - jnp.exp(steps * jnp.log(jnp.full((8, 128), BETA_ONE))))
    bias_two = jnp.max(1.0 - jnp.exp(steps * jnp.log(jnp.full((8, 128), BETA_TWO))))
    for shift in range(4):
        base = ((where[4] - shift) & 3) * OWN
        for k in range(OWN):
            state = states[shift]
            master = state[k]
            grad = grads[shift][k] * clip
            first = BETA_ONE * state[OWN + k] + (1.0 - BETA_ONE) * grad
            second = BETA_TWO * state[2 * OWN + k] + (1.0 - BETA_TWO) * grad * grad
            update = first / bias_one / (jnp.sqrt(second / bias_two) + ADAM_EPS)
            moved = master - LEARN_RATE * (update + WEIGHT_DECAY * master)
            if shift == 0:
                new_master[k] = moved
                encode(first, fcode, fscale, fpower, k)
                encode(second, scode, sscale, spower, k)
            largest = jnp.max(jnp.abs(moved)) + EPSILON
            scale = jnp.full((8, 128), largest).astype(jnp.bfloat16).astype(jnp.float32)
            scale = jnp.max(scale)
            wscale[base + k] = scale
            wcode[base + k] = (moved / scale).astype(wcode.dtype)


def finish(numel, where, step, squares, grads, states):
    tile = grads[0].shape[1:]
    f32, bf16 = jnp.float32, jnp.bfloat16

    def body(*refs):
        finish_kernel(numel, *refs)

    shapes = [
        ((OWN, *tile), f32, VMEM),
        ((OWN, *tile), bf16, VMEM),
        ((OWN,), f32, SMEM),
        ((OWN,), f32, SMEM),
        ((OWN, *tile), bf16, VMEM),
        ((OWN,), f32, SMEM),
        ((OWN,), f32, SMEM),
        ((4 * OWN, *tile), bf16, VMEM),
        ((4 * OWN,), f32, SMEM),
    ]
    return pl.pallas_call(
        body,
        out_shape=[jax.ShapeDtypeStruct(s, d) for s, d, _ in shapes],
        in_specs=[pl.BlockSpec(memory_space=SMEM)] * 2 + [pl.BlockSpec(memory_space=VMEM)] * 9,
        out_specs=[pl.BlockSpec(memory_space=m) for _, _, m in shapes],
        name="finish",
    )(where, step, squares, *grads, *states)


def on_device(
    gradients,
    owner_table,
    step_count,
    master,
    first_code,
    first_scale,
    first_power,
    second_code,
    second_scale,
    second_power,
):
    f32, bf16 = jnp.float32, jnp.bfloat16
    devices = 256
    numel = float(devices * master.size)
    place = [lax.axis_index(a) for a in ("y", "zh", "zl", "core", "expert")]
    table = owner_table[0]
    grads = gradients[0]
    mine = jnp.stack(place).astype(jnp.int32)
    theirs = jnp.stack(place[:3] + [1 - place[3], place[4]]).astype(jnp.int32)

    leaving = pick(theirs, table, grads)
    from_core = [lax.ppermute(t, "core", [(0, 1), (1, 0)]) for t in leaving]
    kept = pick(mine, table, grads)

    state = decode(
        first_scale, first_power, second_scale, second_power, master, first_code, second_code
    )
    states = [state] + [lax.ppermute(state, "expert", shifted(4, s)) for s in (1, 2, 3)]

    held = [[kept[k], from_core[k]] for k in range(OWN)]

    def added(k, start, stop):
        longest = held[k][0].shape[0]
        return sum(
            p[p.shape[0] - longest + start : p.shape[0] - longest + stop].astype(f32)
            for p in held[k]
        )

    start, size = 0, 16
    for step in range(3):
        arrived = []
        for k in range(OWN):
            axis, pairs = STEPS[k][step]
            sent = added(k, start, start + size).astype(bf16)
            arrived.append(lax.ppermute(sent, axis, pairs))
        for k in range(OWN):
            held[k].append(arrived[k])
        start, size = start + size, size // 2
    last = []
    for shift in (1, 2, 3):
        sent = jnp.concatenate(
            [added(k, 28 + shift, 29 + shift).astype(bf16) for k in range(OWN)]
        )
        last.append(lax.ppermute(sent, "zh", shifted(4, shift)))
    rests = [added(k, 28, 29)[0] for k in range(OWN)]
    owned, rows = total(rests, last, devices)
    squares = lax.all_to_all(rows, EVERY, split_axis=0, concat_axis=0, tiled=True)
    sums = [owned] + [lax.ppermute(owned, "expert", shifted(4, s)) for s in (1, 2, 3)]
    squares = squares.reshape(devices, -1)
    outs = finish(numel, mine, step_count, squares, sums, states)
    return (*outs[:8], outs[8].astype(bf16))


def solution(mesh):
    split = Mesh(
        mesh.devices.reshape(4, 4, 2, 2, mesh.shape["expert"]), EVERY
    )
    tiles = P(DP_EXPERT, None, None)
    each = P(DP_EXPERT)
    return jax.shard_map(
        on_device,
        mesh=split,
        in_specs=(
            P(DP, "expert", None, None),
            P("expert", None),
            P(),
            tiles,
            tiles,
            each,
            each,
            tiles,
            each,
            each,
        ),
        out_specs=(
            tiles,
            tiles,
            each,
            each,
            tiles,
            each,
            each,
            P(DP, None, None),
            P(DP),
        ),
        check_vma=False,
    )
```

time: 285 us -> 138 us (0.48)
  waiting for transfers between devices: 185 us -> 35.1 us
  starting transfers between devices: 13.5 us -> 63 us
  blocking collectives: 48.5 us -> 0 us
  Pallas kernels: 0 us -> 17.8 us
  local copies, waits for them, and re-layouts: 14.7 us -> 2.82 us
    all_to_all x1, waiting for transfers between devices: 185 us -> 12 us  [on_device(): lax.all_to_all(rows, EVERY, split_axis=0, concat_axis=0, tiled=True)]
    ppermute x0 -> x25, starting transfers between devices: none -> 44.8 us  [the longest x12 24 us: on_device(): arrived.append(lax.ppermute(sent, axis, pairs))]
    psum x4 -> x0, blocking collectives: 38.3 us -> none  [over_axes(): array = lax.psum(array, axis)]
    ppermute x0 -> x25, waiting for transfers between devices: none -> 23.1 us  [the longest x12 20.7 us: on_device(): arrived.append(lax.ppermute(sent, axis, pairs))]
    pallas_call x0 -> x5, Pallas kernels: none -> 17.8 us  [the longest x2 8.41 us: pick(): pl.pallas_call(pick_kernel, out_shape=[jax.ShapeDtypeStruct((count, *tile...]
    gather x1 -> x0, local copies, waits for them, and re-layouts: 12 us -> none  [on_device(): permuted = jnp.take(gradients[0], table_row, axis=0)]
    convert_element_type x2 -> x17, other arithmetic: 1.65 us -> 12.8 us  [the longest x12 9.76 us: on_device(): sent = added(k, start, start + size).astype(bf16)]
    all_gather x1 -> x0, blocking collectives: 10.3 us -> none  [sent_together(): lax.all_gather(both, axis, axis=dim, tiled=True)]
  transfers between devices with their start and end apart: 1 -> 26, of which waited for: 1 -> 10; matrix products, arithmetic and copies ran while one was open for 0% -> 12% of each run, Pallas kernels for 0% -> 6%
where the time goes in v1:
time: 138 us; the launch traced here: 137 us
  starting transfers between devices  63 us (46%)
  waiting for transfers between devices  35.1 us (25%)
  Pallas kernels  17.8 us (13%)
  other arithmetic  17 us (12%)
  local copies, waits for them, and re-layouts  2.82 us (2%)
  between operations  1.61 us (1%)
    ppermute x12, starting transfers between devices, on_device(): arrived.append(lax.ppermute(sent, axis, pairs))  24 us
    ppermute x12, waiting for transfers between devices, on_device(): arrived.append(lax.ppermute(sent, axis, pairs))  20.7 us
    all_to_all x1, starting transfers between devices, on_device(): lax.all_to_all(rows, EVERY, split_axis=0, concat_axis=0, tiled=True)  18.2 us
    all_to_all x1, waiting for transfers between devices, on_device(): lax.all_to_all(rows, EVERY, split_axis=0, concat_axis=0, tiled=True)  12 us
    convert_element_type x12, other arithmetic, on_device(): sent = added(k, start, start + size).astype(bf16)  9.76 us
    pallas_call x2, Pallas kernels, pick(): pl.pallas_call(pick_kernel, out_shape=[jax.ShapeDtypeStruct((count, *tile...  8.41 us
    ppermute x3, starting transfers between devices, on_device(): last.append(lax.ppermute(sent, 'zh', shifted(4, shift)))  7.68 us
    ppermute x3, starting transfers between devices, on_device(): lax.ppermute(owned, 'expert', shifted(4, s))  5.85 us
  transfers between devices with their start and end apart: 26, of which 10 were waited for; matrix products, arithmetic and copies ran while one was open for 12% of the time, Pallas kernels for 6%

profile of v1, /device:TPU:1, one launch (start us, length us, event | category | flops | bytes accessed | tf_op | source)
XLA Modules:
  0.0 137.2 jit_solution(11078299249681855497)
XLA Ops:
  0.7 0.6 stack.35.where
  1.3 4.2 %pick.3 = (bf16[32,128,128]{2,1,0:T(8,128)(2,1)}, bf16[32,128,128]{2,1,0:T(8,128)(2,1)}, bf16[32,128,128]{2,1,0:T(8,128)(2,1)}, bf16[32,128,128]{2,1,0:T(8,128)(2,1)}) custom-call(s32[5]{0:T(128)} %stack.35.where, s32[256]{0:T(256)} %bitcast.20, bf16[256,128,128]{2,1,0:T(8,128)(2,1)} %bitcast.17), custom_call_target="tpu_custom_call" | custom-call | tf_op jit(solution)/shard_map/pick/pallas_call | solution.py:84
  5.5 3.3 %collective-permute-start = (bf16[32,128,128]{2,1,0:T(8,128)(2,1)}, bf16[32,128,128]{2,1,0:T(8,128)(2,1)}, u32[]{:S(2)}, u32[]{:S(2)}) collective-permute-start(bf16[32,128,128]{2,1,0:T(8,128)(2,1)} %get-tuple-element.29), channel_id=1, source_target_pairs={{0,4},{4,0},{1,5},{5,1},{2,6},{6,2},{3,7},{7,3},{8,12},{12,8},{9,1... | collective-permute-start | bytes 3145736 | tf_op jit(solution)/shard_map/ppermute | solution.py:245
  9.4 2.1 %decode.1.refs_7_ = f32[12,128,128]{2,1,0:T(8,128)} custom-call(f32[4]{0:T(128)} %fs.1, f32[4]{0:T(128)} %fp.1, f32[4]{0:T(128)} %ss.1, f32[4]{0:T(128)} %sp.1, f32[4,128,128]{2,1,0:T(8,128)} %master.1, bf16[4,128,128]{2,1,0:T(8,128)(2,1)} %first_code.1, bf16[4,128,128]{2,1,0:T(8,128)(2,1)} %second_code.1), custom_call_target="tpu_custom_call" | custom-call | tf_op jit(solution)/shard_map/decode/pallas_call | solution.py:116
  11.5 0.6 stack.33.where.refs_0_
  12.1 4.2 %pick.2 = (bf16[32,128,128]{2,1,0:T(8,128)(2,1)}, bf16[32,128,128]{2,1,0:T(8,128)(2,1)}, bf16[32,128,128]{2,1,0:T(8,128)(2,1)}, bf16[32,128,128]{2,1,0:T(8,128)(2,1)}) custom-call(s32[5]{0:T(128)} %stack.33.where.refs_0_, s32[256]{0:T(256)} %bitcast.21, bf16[256,128,128]{2,1,0:T(8,128)(2,1)} %bitcast.18), custom_call_target="tpu_custom_call" | custom-call | tf_op jit(solution)/shard_map/pick/pallas_call | solution.py:84
  16.4 2.0 %collective-permute-start.23 = (f32[12,128,128]{2,1,0:T(8,128)S(1)}, f32[12,128,128]{2,1,0:T(8,128)}, u32[]{:S(2)}, u32[]{:S(2)}) collective-permute-start(f32[12,128,128]{2,1,0:T(8,128)S(1)} %copy-done), channel_id=1, source_target_pairs={{0,2},{1,3},{2,0},{3,1},{4,6},{5,7},{6,4},{7,5},{8,10},{9,11},{10,... | collective-permute-start | bytes 2359304 | tf_op jit(solution)/shard_map/ppermute | solution.py:251
  18.4 1.3 add_convert_fusion.3
  19.8 1.4 %collective-permute-start.1 = (bf16[16,128,128]{2,1,0:T(8,128)(2,1)S(1)}, bf16[16,128,128]{2,1,0:T(8,128)(2,1)S(1)}, u32[]{:S(2)}, u32[]{:S(2)}) collective-permute-start(bf16[16,128,128]{2,1,0:T(8,128)(2,1)S(1)} %add_convert_fusion.3), channel_id=1, source_target_pairs={{0,64},{64,0},{128,192},{192,128},{1,65},{65,1},{129,193},{193,129... | collective-permute-start | bytes 1572872 | tf_op jit(solution)/shard_map/ppermute | solution.py:268
  21.2 1.3 add_convert_fusion.2
  22.5 2.0 %collective-permute-start.5 = (bf16[16,128,128]{2,1,0:T(8,128)(2,1)S(1)}, bf16[16,128,128]{2,1,0:T(8,128)(2,1)S(1)}, u32[]{:S(2)}, u32[]{:S(2)}) collective-permute-start(bf16[16,128,128]{2,1,0:T(8,128)(2,1)S(1)} %add_convert_fusion.2), channel_id=1, source_target_pairs={{0,192},{64,128},{128,64},{192,0},{1,193},{65,129},{129,65},{193,1... | collective-permute-start | bytes 1572872 | tf_op jit(solution)/shard_map/ppermute | solution.py:268
  24.5 1.2 add_convert_fusion.1
  25.7 1.7 %collective-permute-start.9 = (bf16[16,128,128]{2,1,0:T(8,128)(2,1)S(1)}, bf16[16,128,128]{2,1,0:T(8,128)(2,1)S(1)}, u32[]{:S(2)}, u32[]{:S(2)}) collective-permute-start(bf16[16,128,128]{2,1,0:T(8,128)(2,1)S(1)} %add_convert_fusion.1), channel_id=1, source_target_pairs={{0,8},{8,0},{16,24},{24,16},{32,40},{40,32},{48,56},{56,48},{1,9},... | collective-permute-start | bytes 1572872 | tf_op jit(solution)/shard_map/ppermute | solution.py:268
  27.4 1.2 add_convert_fusion
  28.6 3.9 %collective-permute-done.1 = bf16[16,128,128]{2,1,0:T(8,128)(2,1)S(1)} collective-permute-done((bf16[16,128,128]{2,1,0:T(8,128)(2,1)S(1)}, bf16[16,128,128]{2,1,0:T(8,128)(2,1)S(1)}, u32[]{:S(2)}, u32[]{:S(2)}) %collective-permute-start.1) | collective-permute-done | bytes 524320 | tf_op jit(solution)/shard_map/ppermute | solution.py:268
  32.5 5.5 %collective-permute-start.13 = (bf16[16,128,128]{2,1,0:T(8,128)(2,1)S(1)}, bf16[16,128,128]{2,1,0:T(8,128)(2,1)S(1)}, u32[]{:S(2)}, u32[]{:S(2)}) collective-permute-start(bf16[16,128,128]{2,1,0:T(8,128)(2,1)S(1)} %add_convert_fusion), channel_id=1, source_target_pairs={{0,56},{8,16},{16,8},{24,32},{32,24},{40,48},{48,40},{56,0},{1,57}... | collective-permute-start | bytes 1572872 | tf_op jit(solution)/shard_map/ppermute | solution.py:268
  38.0 1.1 add_convert_fusion.7
  39.1 1.3 collective-permute-start.24
  40.4 1.1 add_convert_fusion.6
  41.8 6.7 %collective-permute-done.13 = bf16[16,128,128]{2,1,0:T(8,128)(2,1)S(1)} collective-permute-done((bf16[16,128,128]{2,1,0:T(8,128)(2,1)S(1)}, bf16[16,128,128]{2,1,0:T(8,128)(2,1)S(1)}, u32[]{:S(2)}, u32[]{:S(2)}) %collective-permute-start.13) | collective-permute-done | bytes 524320 | tf_op jit(solution)/shard_map/ppermute | solution.py:268
  48.5 2.4 %collective-permute-start.6 = (bf16[8,128,128]{2,1,0:T(8,128)(2,1)S(1)}, bf16[8,128,128]{2,1,0:T(8,128)(2,1)S(1)}, u32[]{:S(2)}, u32[]{:S(2)}) collective-permute-start(bf16[8,128,128]{2,1,0:T(8,128)(2,1)S(1)} %add_convert_fusion.6), channel_id=1, source_target_pairs={{0,56},{8,16},{16,8},{24,32},{32,24},{40,48},{48,40},{56,0},{1,57}... | collective-permute-start | bytes 786440 | tf_op jit(solution)/shard_map/ppermute | solution.py:268
  51.0 2.8 %collective-permute-start.14 = (bf16[8,128,128]{2,1,0:T(8,128)(2,1)S(1)}, bf16[8,128,128]{2,1,0:T(8,128)(2,1)S(1)}, u32[]{:S(2)}, u32[]{:S(2)}) collective-permute-start(bf16[8,128,128]{2,1,0:T(8,128)(2,1)S(1)} %add_convert_fusion.4), channel_id=1, source_target_pairs={{0,192},{64,128},{128,64},{192,0},{1,193},{65,129},{129,65},{193,1... | collective-permute-start | bytes 786440 | tf_op jit(solution)/shard_map/ppermute | solution.py:268
  53.9 1.0 add_convert_fusion.11
  55.3 1.3 collective-permute-start.10
  56.6 1.0 add_convert_fusion.10
  57.9 2.7 %collective-permute-start.3 = (bf16[4,128,128]{2,1,0:T(8,128)(2,1)S(1)}, bf16[4,128,128]{2,1,0:T(8,128)(2,1)S(1)}, u32[]{:S(2)}, u32[]{:S(2)}) collective-permute-start(bf16[4,128,128]{2,1,0:T(8,128)(2,1)S(1)} %add_convert_fusion.11), channel_id=1, source_target_pairs={{0,192},{64,128},{128,64},{192,0},{1,193},{65,129},{129,65},{193,1... | collective-permute-start | bytes 393224 | tf_op jit(solution)/shard_map/ppermute | solution.py:268
  60.8 1.0 collective-permute-start.15
  61.9 3.6 %collective-permute-done.15 = bf16[4,128,128]{2,1,0:T(8,128)(2,1)S(1)} collective-permute-done((bf16[4,128,128]{2,1,0:T(8,128)(2,1)S(1)}, bf16[4,128,128]{2,1,0:T(8,128)(2,1)S(1)}, u32[]{:S(2)}, u32[]{:S(2)}) %collective-permute-start.15) | collective-permute-done | bytes 131104 | tf_op jit(solution)/shard_map/ppermute | solution.py:268
  65.5 2.7 %collective-permute-start.11 = (bf16[4,128,128]{2,1,0:T(8,128)(2,1)S(1)}, bf16[4,128,128]{2,1,0:T(8,128)(2,1)S(1)}, u32[]{:S(2)}, u32[]{:S(2)}) collective-permute-start(bf16[4,128,128]{2,1,0:T(8,128)(2,1)S(1)} %add_convert_fusion.9), channel_id=1, source_target_pairs={{0,192},{64,128},{128,64},{192,0},{1,193},{65,129},{129,65},{193,1... | collective-permute-start | bytes 393224 | tf_op jit(solution)/shard_map/ppermute | solution.py:268
  68.4 2.3 %collective-permute-done.11 = bf16[4,128,128]{2,1,0:T(8,128)(2,1)S(1)} collective-permute-done((bf16[4,128,128]{2,1,0:T(8,128)(2,1)S(1)}, bf16[4,128,128]{2,1,0:T(8,128)(2,1)S(1)}, u32[]{:S(2)}, u32[]{:S(2)}) %collective-permute-start.11) | collective-permute-done | bytes 131104 | tf_op jit(solution)/shard_map/ppermute | solution.py:268
  71.1 3.3 %collective-permute-done.7 = bf16[4,128,128]{2,1,0:T(8,128)(2,1)S(1)} collective-permute-done((bf16[4,128,128]{2,1,0:T(8,128)(2,1)S(1)}, bf16[4,128,128]{2,1,0:T(8,128)(2,1)S(1)}, u32[]{:S(2)}, u32[]{:S(2)}) %collective-permute-start.7) | collective-permute-done | bytes 131104 | tf_op jit(solution)/shard_map/ppermute | solution.py:268
  74.5 0.9 add_convert_fusion.14
  75.4 0.9 add_convert_fusion.15
  76.4 4.0 %collective-permute-start.17 = (bf16[4,128,128]{2,1,0:T(8,128)(2,1)S(1)}, bf16[4,128,128]{2,1,0:T(8,128)(2,1)S(1)}, u32[]{:S(2)}, u32[]{:S(2)}) collective-permute-start(bf16[4,128,128]{2,1,0:T(8,128)(2,1)S(1)} %pad_maximum_fusion.1), channel_id=1, source_target_pairs={{0,32},{16,48},{32,0},{48,16},{1,33},{17,49},{33,1},{49,17},{2,34}... | collective-permute-start | bytes 393224 | tf_op jit(solution)/shard_map/ppermute | solution.py:277
  80.4 1.4 %add_bitcast_fusion.3.refs_0_ = f32[128,128]{1,0:T(8,128)} fusion(bf16[4,128,128]{2,1,0:T(8,128)(2,1)S(1)} %collective-permute-done.3, bf16[8,128,128]{2,1,0:T(8,128)(2,1)S(1)} %collective-permute-done.2, bf16[16,128,128]{2,1,0:T(8,128)(2,1)S(1)} %collective-permute-done.1, bf16[32,128,128]{2,1,0:T(8,128)(2,1)} %collective-permute-done, ...), kind=kLoop, calls=%fused_computation.30 | loop fusion | flops 147456 | bytes 229376 | tf_op jit(solution)/shard_map/squeeze | solution.py:278
  81.8 1.4 %add_bitcast_fusion.2.refs_1_ = f32[128,128]{1,0:T(8,128)} fusion(bf16[4,128,128]{2,1,0:T(8,128)(2,1)S(1)} %collective-permute-done.7, bf16[8,128,128]{2,1,0:T(8,128)(2,1)S(1)} %collective-permute-done.6, bf16[16,128,128]{2,1,0:T(8,128)(2,1)S(1)} %collective-permute-done.5, bf16[32,128,128]{2,1,0:T(8,128)(2,1)} %collective-permute-done.4, ...), kind=kLoop, calls=%fused_computation.29 | loop fusion | flops 147456 | bytes 229376 | tf_op jit(solution)/shard_map/squeeze | solution.py:278
  83.2 0.7 add_bitcast_fusion.1.refs_2_
  83.9 3.6 %collective-permute-start.18 = (bf16[4,128,128]{2,1,0:T(8,128)(2,1)S(1)}, bf16[4,128,128]{2,1,0:T(8,128)(2,1)S(1)}, u32[]{:S(2)}, u32[]{:S(2)}) collective-permute-start(bf16[4,128,128]{2,1,0:T(8,128)(2,1)S(1)} %pad_maximum_fusion.2), channel_id=1, source_target_pairs={{0,48},{16,0},{32,16},{48,32},{1,49},{17,1},{33,17},{49,33},{2,50}... | collective-permute-start | bytes 393224 | tf_op jit(solution)/shard_map/ppermute | solution.py:277
  87.6 0.7 add_bitcast_fusion.refs_3_
  88.2 2.4 %collective-permute-done.18.refs_6_ = bf16[4,128,128]{2,1,0:T(8,128)(2,1)S(1)} collective-permute-done((bf16[4,128,128]{2,1,0:T(8,128)(2,1)S(1)}, bf16[4,128,128]{2,1,0:T(8,128)(2,1)S(1)}, u32[]{:S(2)}, u32[]{:S(2)}) %collective-permute-start.18) | collective-permute-done | bytes 131104 | tf_op jit(solution)/shard_map/ppermute | solution.py:277
  90.6 0.7 copy-done.9
  91.3 2.0 %total.1 = (f32[4,128,128]{2,1,0:T(8,128)}, f32[256,1,128]{2,1,0:T(1,128)}) custom-call(f32[128,128]{1,0:T(8,128)} %add_bitcast_fusion.3.refs_0_, f32[128,128]{1,0:T(8,128)} %add_bitcast_fusion.2.refs_1_, f32[128,128]{1,0:T(8,128)} %add_bitcast_fusion.1.refs_2_, f32[128,128]{1,0:T(8,128)} %add_bitcast_fusion.refs_3_, bf16[4,128,128]{2,1,0:T(8,128)(2,1)} %copy-done.7, ...), custom_call_target="tpu_custom_call" | custom-call | tf_op jit(solution)/shard_map/total/pallas_call | solution.py:139
  93.3 5.8 %collective-permute-start.20 = (f32[4,128,128]{2,1,0:T(8,128)}, f32[4,128,128]{2,1,0:T(8,128)S(1)}, u32[]{:S(2)}, u32[]{:S(2)}) collective-permute-start(f32[4,128,128]{2,1,0:T(8,128)} %get-tuple-element.37.refs_3_), channel_id=1, source_target_pairs={{0,2},{1,3},{2,0},{3,1},{4,6},{5,7},{6,4},{7,5},{8,10},{9,11},{10,... | collective-permute-start | bytes 786440 | tf_op jit(solution)/shard_map/ppermute | solution.py:281
  99.1 18.2 %all-to-all-start = ((f32[256,1,128]{2,1,0:T(1,128)}), f32[256,1,128]{2,1,0:T(1,128)S(1)}, u32[]{:S(2)}, u32[]{:S(2)}) async-start(f32[256,1,128]{2,1,0:T(1,128)} %get-tuple-element.36), calls=%async_computation | async-start | bytes 262144 | tf_op jit(solution)/shard_map/all_to_all | solution.py:280
  118.0 12.0 %all-to-all-done = f32[256,1,128]{2,1,0:T(1,128)S(1)} async-done(((f32[256,1,128]{2,1,0:T(1,128)}), f32[256,1,128]{2,1,0:T(1,128)S(1)}, u32[]{:S(2)}, u32[]{:S(2)}) %all-to-all-start) | async-done | bytes 131104 | tf_op jit(solution)/shard_map/all_to_all | solution.py:280
  130.0 0.6 copy-done.3
  130.9 5.3 %finish.1 = (f32[4,128,128]{2,1,0:T(8,128)}, bf16[4,128,128]{2,1,0:T(8,128)(2,1)}, f32[4]{0:T(128)}, f32[4]{0:T(128)}, bf16[4,128,128]{2,1,0:T(8,128)(2,1)}, /*i...) custom-call(s32[5]{0:T(128)} %stack.33.where.refs_0_, s32[1]{0:T(128)S(6)} %copy.20.refs_1_, ...), custom_call_target="tpu_custom_call" | custom-call | tf_op jit(solution)/shard_map/finish/pallas_call | solution.py:214
  136.2 1.1 convert_element_type.563
  (55 shorter events, 3.0 us)
Async XLA Ops:
  5.5 10.9 %collective-permute-start = (bf16[32,128,128]{2,1,0:T(8,128)(2,1)}, bf16[32,128,128]{2,1,0:T(8,128)(2,1)}, u32[]{:S(2)}, u32[]{:S(2)}) collective-permute-start(bf16[32,128,128]{2,1,0:T(8,128)(2,1)} %get-tuple-element.29), channel_id=1, source_target_pairs={{0,4},{4,0},{1,5},{5,1},{2,6},{6,2},{3,7},{7,3},{8,12},{12,8},{9,1... | collective-permute-start | bytes 3145736 | tf_op jit(solution)/shard_map/ppermute | solution.py:245
  8.8 11.0 %collective-permute-start.4 = (bf16[32,128,128]{2,1,0:T(8,128)(2,1)}, bf16[32,128,128]{2,1,0:T(8,128)(2,1)}, u32[]{:S(2)}, u32[]{:S(2)}) collective-permute-start(bf16[32,128,128]{2,1,0:T(8,128)(2,1)} %get-tuple-element.31), channel_id=1, source_target_pairs={{0,4},{4,0},{1,5},{5,1},{2,6},{6,2},{3,7},{7,3},{8,12},{12,8},{9,1... | collective-permute-start | bytes 3145736 | tf_op jit(solution)/shard_map/ppermute | solution.py:245
  8.9 13.6 %collective-permute-start.8 = (bf16[32,128,128]{2,1,0:T(8,128)(2,1)}, bf16[32,128,128]{2,1,0:T(8,128)(2,1)S(1)}, u32[]{:S(2)}, u32[]{:S(2)}) collective-permute-start(bf16[32,128,128]{2,1,0:T(8,128)(2,1)} %get-tuple-element.33), channel_id=1, source_target_pairs={{0,4},{4,0},{1,5},{5,1},{2,6},{6,2},{3,7},{7,3},{8,12},{12,8},{9,1... | collective-permute-start | bytes 3145736 | tf_op jit(solution)/shard_map/ppermute | solution.py:245
  9.3 16.4 %collective-permute-start.12 = (bf16[32,128,128]{2,1,0:T(8,128)(2,1)}, bf16[32,128,128]{2,1,0:T(8,128)(2,1)S(1)}, u32[]{:S(2)}, u32[]{:S(2)}) collective-permute-start(bf16[32,128,128]{2,1,0:T(8,128)(2,1)} %get-tuple-element.35), channel_id=1, source_target_pairs={{0,4},{4,0},{1,5},{5,1},{2,6},{6,2},{3,7},{7,3},{8,12},{12,8},{9,1... | collective-permute-start | bytes 3145736 | tf_op jit(solution)/shard_map/ppermute | solution.py:245
  11.5 4.9 %copy-start = (f32[12,128,128]{2,1,0:T(8,128)S(1)}, f32[12,128,128]{2,1,0:T(8,128)}, u32[]{:S(2)}) copy-start(f32[12,128,128]{2,1,0:T(8,128)} %decode.1.refs_7_) | copy-start | bytes 2359300
  11.5 87.6 %collective-permute-start.22 = (f32[12,128,128]{2,1,0:T(8,128)}, f32[12,128,128]{2,1,0:T(8,128)}, u32[]{:S(2)}, u32[]{:S(2)}) collective-permute-start(f32[12,128,128]{2,1,0:T(8,128)} %decode.1.refs_7_), channel_id=1, source_target_pairs={{0,1},{1,2},{2,3},{3,0},{4,5},{5,6},{6,7},{7,4},{8,9},{9,10},{10,1... | collective-permute-start | bytes 2359304 | tf_op jit(solution)/shard_map/ppermute | solution.py:251
  16.3 25.3 %copy-start.2 = (bf16[32,128,128]{2,1,0:T(8,128)(2,1)S(1)}, bf16[32,128,128]{2,1,0:T(8,128)(2,1)}, u32[]{:S(2)}) copy-start(bf16[32,128,128]{2,1,0:T(8,128)(2,1)} %get-tuple-element.32) | copy-start | bytes 3145732
  16.4 34.6 %copy-start.1 = (bf16[32,128,128]{2,1,0:T(8,128)(2,1)S(1)}, bf16[32,128,128]{2,1,0:T(8,128)(2,1)}, u32[]{:S(2)}) copy-start(bf16[32,128,128]{2,1,0:T(8,128)(2,1)} %get-tuple-element.34) | copy-start | bytes 3145732
  16.4 101.5 %collective-permute-start.23 = (f32[12,128,128]{2,1,0:T(8,128)S(1)}, f32[12,128,128]{2,1,0:T(8,128)}, u32[]{:S(2)}, u32[]{:S(2)}) collective-permute-start(f32[12,128,128]{2,1,0:T(8,128)S(1)} %copy-done), channel_id=1, source_target_pairs={{0,2},{1,3},{2,0},{3,1},{4,6},{5,7},{6,4},{7,5},{8,10},{9,11},{10,... | collective-permute-start | bytes 2359304 | tf_op jit(solution)/shard_map/ppermute | solution.py:251
  19.8 12.7 %collective-permute-start.1 = (bf16[16,128,128]{2,1,0:T(8,128)(2,1)S(1)}, bf16[16,128,128]{2,1,0:T(8,128)(2,1)S(1)}, u32[]{:S(2)}, u32[]{:S(2)}) collective-permute-start(bf16[16,128,128]{2,1,0:T(8,128)(2,1)S(1)} %add_convert_fusion.3), channel_id=1, source_target_pairs={{0,64},{64,0},{128,192},{192,128},{1,65},{65,1},{129,193},{193,129... | collective-permute-start | bytes 1572872 | tf_op jit(solution)/shard_map/ppermute | solution.py:268
  22.5 16.6 %collective-permute-start.5 = (bf16[16,128,128]{2,1,0:T(8,128)(2,1)S(1)}, bf16[16,128,128]{2,1,0:T(8,128)(2,1)S(1)}, u32[]{:S(2)}, u32[]{:S(2)}) collective-permute-start(bf16[16,128,128]{2,1,0:T(8,128)(2,1)S(1)} %add_convert_fusion.2), channel_id=1, source_target_pairs={{0,192},{64,128},{128,64},{192,0},{1,193},{65,129},{129,65},{193,1... | collective-permute-start | bytes 1572872 | tf_op jit(solution)/shard_map/ppermute | solution.py:268
  25.7 15.9 %collective-permute-start.9 = (bf16[16,128,128]{2,1,0:T(8,128)(2,1)S(1)}, bf16[16,128,128]{2,1,0:T(8,128)(2,1)S(1)}, u32[]{:S(2)}, u32[]{:S(2)}) collective-permute-start(bf16[16,128,128]{2,1,0:T(8,128)(2,1)S(1)} %add_convert_fusion.1), channel_id=1, source_target_pairs={{0,8},{8,0},{16,24},{24,16},{32,40},{40,32},{48,56},{56,48},{1,9},... | collective-permute-start | bytes 1572872 | tf_op jit(solution)/shard_map/ppermute | solution.py:268
  32.5 16.0 %collective-permute-start.13 = (bf16[16,128,128]{2,1,0:T(8,128)(2,1)S(1)}, bf16[16,128,128]{2,1,0:T(8,128)(2,1)S(1)}, u32[]{:S(2)}, u32[]{:S(2)}) collective-permute-start(bf16[16,128,128]{2,1,0:T(8,128)(2,1)S(1)} %add_convert_fusion), channel_id=1, source_target_pairs={{0,56},{8,16},{16,8},{24,32},{32,24},{40,48},{48,40},{56,0},{1,57}... | collective-permute-start | bytes 1572872 | tf_op jit(solution)/shard_map/ppermute | solution.py:268
  39.1 78.8 %collective-permute-start.24 = (f32[12,128,128]{2,1,0:T(8,128)S(1)}, f32[12,128,128]{2,1,0:T(8,128)}, u32[]{:S(2)}, u32[]{:S(2)}) collective-permute-start(f32[12,128,128]{2,1,0:T(8,128)S(1)} %copy-done), channel_id=1, source_target_pairs={{0,3},{1,0},{2,1},{3,2},{4,7},{5,4},{6,5},{7,6},{8,11},{9,8},{10,9... | collective-permute-start | bytes 2359304 | tf_op jit(solution)/shard_map/ppermute | solution.py:251
  41.6 9.5 %collective-permute-start.2 = (bf16[8,128,128]{2,1,0:T(8,128)(2,1)S(1)}, bf16[8,128,128]{2,1,0:T(8,128)(2,1)S(1)}, u32[]{:S(2)}, u32[]{:S(2)}) collective-permute-start(bf16[8,128,128]{2,1,0:T(8,128)(2,1)S(1)} %add_convert_fusion.7), channel_id=1, source_target_pairs={{0,8},{8,0},{16,24},{24,16},{32,40},{40,32},{48,56},{56,48},{1,9},... | collective-permute-start | bytes 786440 | tf_op jit(solution)/shard_map/ppermute | solution.py:268
  48.5 6.8 %collective-permute-start.6 = (bf16[8,128,128]{2,1,0:T(8,128)(2,1)S(1)}, bf16[8,128,128]{2,1,0:T(8,128)(2,1)S(1)}, u32[]{:S(2)}, u32[]{:S(2)}) collective-permute-start(bf16[8,128,128]{2,1,0:T(8,128)(2,1)S(1)} %add_convert_fusion.6), channel_id=1, source_target_pairs={{0,56},{8,16},{16,8},{24,32},{32,24},{40,48},{48,40},{56,0},{1,57}... | collective-permute-start | bytes 786440 | tf_op jit(solution)/shard_map/ppermute | solution.py:268
  51.0 6.9 %collective-permute-start.14 = (bf16[8,128,128]{2,1,0:T(8,128)(2,1)S(1)}, bf16[8,128,128]{2,1,0:T(8,128)(2,1)S(1)}, u32[]{:S(2)}, u32[]{:S(2)}) collective-permute-start(bf16[8,128,128]{2,1,0:T(8,128)(2,1)S(1)} %add_convert_fusion.4), channel_id=1, source_target_pairs={{0,192},{64,128},{128,64},{192,0},{1,193},{65,129},{129,65},{193,1... | collective-permute-start | bytes 786440 | tf_op jit(solution)/shard_map/ppermute | solution.py:268
  55.3 5.5 %collective-permute-start.10 = (bf16[8,128,128]{2,1,0:T(8,128)(2,1)S(1)}, bf16[8,128,128]{2,1,0:T(8,128)(2,1)S(1)}, u32[]{:S(2)}, u32[]{:S(2)}) collective-permute-start(bf16[8,128,128]{2,1,0:T(8,128)(2,1)S(1)} %add_convert_fusion.5), channel_id=1, source_target_pairs={{0,64},{64,0},{128,192},{192,128},{1,65},{65,1},{129,193},{193,129... | collective-permute-start | bytes 786440 | tf_op jit(solution)/shard_map/ppermute | solution.py:268
  57.9 17.4 %collective-permute-start.3 = (bf16[4,128,128]{2,1,0:T(8,128)(2,1)S(1)}, bf16[4,128,128]{2,1,0:T(8,128)(2,1)S(1)}, u32[]{:S(2)}, u32[]{:S(2)}) collective-permute-start(bf16[4,128,128]{2,1,0:T(8,128)(2,1)S(1)} %add_convert_fusion.11), channel_id=1, source_target_pairs={{0,192},{64,128},{128,64},{192,0},{1,193},{65,129},{129,65},{193,1... | collective-permute-start | bytes 393224 | tf_op jit(solution)/shard_map/ppermute | solution.py:268
  60.8 4.7 %collective-permute-start.15 = (bf16[4,128,128]{2,1,0:T(8,128)(2,1)S(1)}, bf16[4,128,128]{2,1,0:T(8,128)(2,1)S(1)}, u32[]{:S(2)}, u32[]{:S(2)}) collective-permute-start(bf16[4,128,128]{2,1,0:T(8,128)(2,1)S(1)} %add_convert_fusion.8), channel_id=1, source_target_pairs={{0,64},{64,0},{128,192},{192,128},{1,65},{65,1},{129,193},{193,129... | collective-permute-start | bytes 393224 | tf_op jit(solution)/shard_map/ppermute | solution.py:268
  65.5 5.1 %collective-permute-start.11 = (bf16[4,128,128]{2,1,0:T(8,128)(2,1)S(1)}, bf16[4,128,128]{2,1,0:T(8,128)(2,1)S(1)}, u32[]{:S(2)}, u32[]{:S(2)}) collective-permute-start(bf16[4,128,128]{2,1,0:T(8,128)(2,1)S(1)} %add_convert_fusion.9), channel_id=1, source_target_pairs={{0,192},{64,128},{128,64},{192,0},{1,193},{65,129},{129,65},{193,1... | collective-permute-start | bytes 393224 | tf_op jit(solution)/shard_map/ppermute | solution.py:268
  70.6 3.8 %collective-permute-start.7 = (bf16[4,128,128]{2,1,0:T(8,128)(2,1)S(1)}, bf16[4,128,128]{2,1,0:T(8,128)(2,1)S(1)}, u32[]{:S(2)}, u32[]{:S(2)}) collective-permute-start(bf16[4,128,128]{2,1,0:T(8,128)(2,1)S(1)} %add_convert_fusion.10), channel_id=1, source_target_pairs={{0,64},{64,0},{128,192},{192,128},{1,65},{65,1},{129,193},{193,129... | collective-permute-start | bytes 393224 | tf_op jit(solution)/shard_map/ppermute | solution.py:268
  76.3 7.6 %collective-permute-start.16 = (bf16[4,128,128]{2,1,0:T(8,128)(2,1)S(1)}, bf16[4,128,128]{2,1,0:T(8,128)(2,1)S(1)}, u32[]{:S(2)}, u32[]{:S(2)}) collective-permute-start(bf16[4,128,128]{2,1,0:T(8,128)(2,1)S(1)} %pad_maximum_fusion), channel_id=1, source_target_pairs={{0,16},{16,32},{32,48},{48,0},{1,17},{17,33},{33,49},{49,1},{2,18}... | collective-permute-start | bytes 393224 | tf_op jit(solution)/shard_map/ppermute | solution.py:277
  76.4 11.8 %collective-permute-start.17 = (bf16[4,128,128]{2,1,0:T(8,128)(2,1)S(1)}, bf16[4,128,128]{2,1,0:T(8,128)(2,1)S(1)}, u32[]{:S(2)}, u32[]{:S(2)}) collective-permute-start(bf16[4,128,128]{2,1,0:T(8,128)(2,1)S(1)} %pad_maximum_fusion.1), channel_id=1, source_target_pairs={{0,32},{16,48},{32,0},{48,16},{1,33},{17,49},{33,1},{49,17},{2,34}... | collective-permute-start | bytes 393224 | tf_op jit(solution)/shard_map/ppermute | solution.py:277
  83.9 6.7 %copy-start.7 = (bf16[4,128,128]{2,1,0:T(8,128)(2,1)}, bf16[4,128,128]{2,1,0:T(8,128)(2,1)S(1)}, u32[]{:S(2)}) copy-start(bf16[4,128,128]{2,1,0:T(8,128)(2,1)S(1)} %collective-permute-done.16.refs_4_) | copy-start | bytes 393220
  83.9 6.7 %collective-permute-start.18 = (bf16[4,128,128]{2,1,0:T(8,128)(2,1)S(1)}, bf16[4,128,128]{2,1,0:T(8,128)(2,1)S(1)}, u32[]{:S(2)}, u32[]{:S(2)}) collective-permute-start(bf16[4,128,128]{2,1,0:T(8,128)(2,1)S(1)} %pad_maximum_fusion.2), channel_id=1, source_target_pairs={{0,48},{16,0},{32,16},{48,32},{1,49},{17,1},{33,17},{49,33},{2,50}... | collective-permute-start | bytes 393224 | tf_op jit(solution)/shard_map/ppermute | solution.py:277
  88.2 2.4 %copy-start.8 = (bf16[4,128,128]{2,1,0:T(8,128)(2,1)}, bf16[4,128,128]{2,1,0:T(8,128)(2,1)S(1)}, u32[]{:S(2)}) copy-start(bf16[4,128,128]{2,1,0:T(8,128)(2,1)S(1)} %collective-permute-done.17.refs_5_) | copy-start | bytes 393220
  90.6 0.7 copy-start.9
  93.3 36.7 %collective-permute-start.19 = (f32[4,128,128]{2,1,0:T(8,128)}, f32[4,128,128]{2,1,0:T(8,128)S(1)}, u32[]{:S(2)}, u32[]{:S(2)}) collective-permute-start(f32[4,128,128]{2,1,0:T(8,128)} %get-tuple-element.37.refs_3_), channel_id=1, source_target_pairs={{0,1},{1,2},{2,3},{3,0},{4,5},{5,6},{6,7},{7,4},{8,9},{9,10},{10,1... | collective-permute-start | bytes 786440 | tf_op jit(solution)/shard_map/ppermute | solution.py:281
  93.3 36.7 %collective-permute-start.20 = (f32[4,128,128]{2,1,0:T(8,128)}, f32[4,128,128]{2,1,0:T(8,128)S(1)}, u32[]{:S(2)}, u32[]{:S(2)}) collective-permute-start(f32[4,128,128]{2,1,0:T(8,128)} %get-tuple-element.37.refs_3_), channel_id=1, source_target_pairs={{0,2},{1,3},{2,0},{3,1},{4,6},{5,7},{6,4},{7,5},{8,10},{9,11},{10,... | collective-permute-start | bytes 786440 | tf_op jit(solution)/shard_map/ppermute | solution.py:281
  99.1 30.9 %collective-permute-start.21 = (f32[4,128,128]{2,1,0:T(8,128)}, f32[4,128,128]{2,1,0:T(8,128)S(1)}, u32[]{:S(2)}, u32[]{:S(2)}) collective-permute-start(f32[4,128,128]{2,1,0:T(8,128)} %get-tuple-element.37.refs_3_), channel_id=1, source_target_pairs={{0,3},{1,0},{2,1},{3,2},{4,7},{5,4},{6,5},{7,6},{8,11},{9,8},{10,9... | collective-permute-start | bytes 786440 | tf_op jit(solution)/shard_map/ppermute | solution.py:281
  99.1 30.8 %all-to-all-start = ((f32[256,1,128]{2,1,0:T(1,128)}), f32[256,1,128]{2,1,0:T(1,128)S(1)}, u32[]{:S(2)}, u32[]{:S(2)}) async-start(f32[256,1,128]{2,1,0:T(1,128)} %get-tuple-element.36), calls=%async_computation | async-start | bytes 262144 | tf_op jit(solution)/shard_map/all_to_all | solution.py:280
  130.0 0.6 copy-start.3
  130.0 0.8 copy-start.4
  130.0 0.9 copy-start.5
  130.0 0.9 copy-start.6

commit v2 on v1

v2 whole, which is shorter than its diff:
```python
import jax
import jax.numpy as jnp
from jax import lax
from jax.experimental import pallas as pl
from jax.experimental.pallas import tpu as pltpu
from jax.sharding import Mesh
from jax.sharding import PartitionSpec as P

DP = ("y", "zh", "zl", "core")
Z = ("zh", "zl")
EVERY = ("y", "zh", "zl", "core", "expert")
DP_EXPERT = EVERY

OWN = 4

BETA_ONE = 0.9
BETA_TWO = 0.95
LEARN_RATE = 0.01
WEIGHT_DECAY = 0.1
CLIP_RMS = 0.5
LOG_SPAN = 4.0
EPSILON = 1e-06
ADAM_EPS = 1e-08

VMEM = pltpu.VMEM
SMEM = pltpu.SMEM

Y_EVEN = [(i, i ^ 1) for i in range(4)]
Y_ODD = [(i, i ^ 3) for i in range(4)]
Z_EVEN = [(i, i ^ 1) for i in range(8)]
Z_ODD = [(i, (i + 1) % 8 if i % 2 else (i - 1) % 8) for i in range(8)]

STEPS = (
    (("y", Y_EVEN), (Z, Z_EVEN), ("y", Y_ODD)),
    (("y", Y_ODD), (Z, Z_ODD), ("y", Y_EVEN)),
    ((Z, Z_EVEN), ("y", Y_EVEN), ("y", Y_ODD)),
    ((Z, Z_ODD), ("y", Y_ODD), ("y", Y_EVEN)),
)


def limit(mib):
    return pltpu.CompilerParams(vmem_limit_bytes=mib * 2**20)


def shifted(count, by):
    return [(i, (i + by) % count) for i in range(count)]


def owner_of(k, place, y, zh, zl):
    bits = ((place >> 4) & 1, (place >> 3) & 1, (place >> 2) & 1)
    shift = place & 3
    for bit, (axis, pairs) in zip(bits, STEPS[k]):
        goes = 1 - bit
        if axis == "y":
            y = y ^ (goes * (1 if pairs is Y_EVEN else 3))
        else:
            if pairs is Z_ODD:
                zh = (zh + goes * (2 * zl - 1)) & 3
            zl = zl ^ goes
    return y, (zh + shift) & 3, zl


def pick_kernel(other, table, grads, *outs):
    y, zh, zl = (lax.axis_index(a) for a in DP[:3])
    core = lax.axis_index("core") ^ other
    for k in range(OWN):

        def move(place, _, k=k):
            oy, ozh, ozl = owner_of(k, place, y, zh, zl)
            slot = ((((oy * 4 + ozh) * 2 + ozl) * 2) + core) * OWN + k
            outs[k][place] = grads[table[slot]]
            return 0

        lax.fori_loop(0, outs[k].shape[0], move, 0, unroll=8)


def pick(other, table, grads):
    tile = grads.shape[1:]
    count = grads.shape[0] // (2 * OWN)

    def body(*refs):
        pick_kernel(other, *refs)

    return pl.pallas_call(
        body,
        out_shape=[VMEM((count, *tile), grads.dtype)] * OWN,
        in_specs=[pl.BlockSpec(memory_space=SMEM), pl.BlockSpec(memory_space=VMEM)],
        out_specs=[pl.BlockSpec(memory_space=VMEM)] * OWN,
        compiler_params=limit(2),
        name="pick",
    )(table, grads)


def in_hbm(arrays):
    return [pltpu.with_memory_space_constraint(a, pltpu.HBM) for a in arrays]


def in_vmem(arrays):
    return [pltpu.with_memory_space_constraint(a, VMEM) for a in arrays]


def root(magnitude, power):
    return jnp.exp(jnp.log(magnitude) * power)


def decode_kernel(fs, fp, ss, sp, master, first_code, second_code, out):
    for i in range(OWN):
        out[i] = master[i]
        for base, code, scale, power in ((OWN, first_code, fs, fp), (2 * OWN, second_code, ss, sp)):
            values = code[i].astype(jnp.float32)
            old = scale[i] * root(jnp.abs(values), 1.0 / jnp.full(values.shape, power[i]))
            out[base + i] = jnp.where(values < 0, -old, old)


def decode(fs, fp, ss, sp, master, first_code, second_code):
    return pl.pallas_call(
        decode_kernel,
        out_shape=jax.ShapeDtypeStruct((3 * OWN, *master.shape[1:]), jnp.float32),
        in_specs=[pl.BlockSpec(memory_space=SMEM)] * 4 + [pl.BlockSpec(memory_space=VMEM)] * 3,
        out_specs=pl.BlockSpec(memory_space=VMEM),
        compiler_params=limit(8),
        name="decode",
    )(fs, fp, ss, sp, master, first_code, second_code)


def total_kernel(*refs):
    parts, (owned, rounded, row) = refs[:-3], refs[-3:]
    squares = jnp.zeros((1, owned.shape[-1]), jnp.float32)
    for k in range(OWN):
        total = parts[k][...]
        for received in parts[OWN:]:
            total = total + received[k].astype(jnp.float32)
        owned[k] = total
        rounded[k] = total.astype(rounded.dtype)
        squares = squares + jnp.sum(total * total, axis=0, keepdims=True)
    row[...] = jnp.broadcast_to(squares[None], row.shape)


def total(rests, received, devices):
    tile = rests[0].shape
    return pl.pallas_call(
        total_kernel,
        out_shape=[
            pltpu.HBM((OWN, *tile), jnp.float32),
            pltpu.HBM((OWN, *tile), jnp.bfloat16),
            pltpu.HBM((devices, 1, tile[-1]), jnp.float32),
        ],
        in_specs=[pl.BlockSpec(memory_space=VMEM)] * (len(rests) + len(received)),
        out_specs=[pl.BlockSpec(memory_space=VMEM)] * 3,
        compiler_params=limit(8),
        name="total",
    )(*in_vmem(rests), *in_vmem(received))


def encode(values, code, scales, powers, i):
    absval = jnp.abs(values)
    largest = jnp.max(absval, axis=(0, 1), keepdims=True)
    average = jnp.sum(absval, axis=(0, 1), keepdims=True) / float(values.shape[0] * values.shape[1])
    power = jnp.clip(LOG_SPAN / jnp.log(1.0 + largest / (average + EPSILON)), 1.0, 3.0)
    scale = largest + EPSILON
    coded = root(absval / scale, power)
    code[i] = jnp.where(values < 0, -coded, coded).astype(code.dtype)
    scales[i] = scale[0, 0]
    powers[i] = power[0, 0]


def finish_kernel(numel, step, squares, *refs):
    grads, states = refs[:4], refs[4:8]
    (new_master, fcode, fscale, fpower, scode, sscale, spower, wcode, wscale) = refs[8:]
    f32 = jnp.float32
    total_sq = jnp.sum(squares[...], axis=(0, 1), keepdims=True)
    clip = jnp.minimum(1.0, CLIP_RMS / jnp.sqrt(total_sq / numel + EPSILON))
    steps = jnp.full((1, 1), step[0]).astype(f32)
    bias_one = 1.0 - jnp.exp(steps * jnp.log(jnp.full((1, 1), BETA_ONE, f32)))
    bias_two = 1.0 - jnp.exp(steps * jnp.log(jnp.full((1, 1), BETA_TWO, f32)))
    lane = lax.broadcasted_iota(jnp.int32, wscale.shape, 1)
    scales = jnp.zeros(wscale.shape, f32)
    for shift in range(4):
        base = ((lax.axis_index("expert") - shift) & 3) * OWN
        for k in range(OWN):
            state = states[shift]
            master = state[k]
            grad = grads[shift][k].astype(f32) * clip
            first = BETA_ONE * state[OWN + k] + (1.0 - BETA_ONE) * grad
            second = BETA_TWO * state[2 * OWN + k] + (1.0 - BETA_TWO) * grad * grad
            update = first / bias_one / (jnp.sqrt(second / bias_two) + ADAM_EPS)
            moved = master - LEARN_RATE * (update + WEIGHT_DECAY * master)
            if shift == 0:
                new_master[k] = moved
                encode(first, fcode, fscale, fpower, k)
                encode(second, scode, sscale, spower, k)
            largest = jnp.max(jnp.abs(moved), axis=(0, 1), keepdims=True) + EPSILON
            scale = largest.astype(jnp.bfloat16).astype(f32)
            scales = jnp.where(lane == base + k, scale, scales)
            wcode[base + k] = (moved / scale).astype(wcode.dtype)
    wscale[...] = scales


def finish(numel, step, squares, grads, states):
    tile = grads[0].shape[1:]
    f32, bf16 = jnp.float32, jnp.bfloat16

    def body(*refs):
        finish_kernel(numel, *refs)

    shapes = [
        ((OWN, *tile), f32, VMEM),
        ((OWN, *tile), bf16, VMEM),
        ((OWN,), f32, SMEM),
        ((OWN,), f32, SMEM),
        ((OWN, *tile), bf16, VMEM),
        ((OWN,), f32, SMEM),
        ((OWN,), f32, SMEM),
        ((4 * OWN, *tile), bf16, VMEM),
    ]
    return pl.pallas_call(
        body,
        out_shape=[jax.ShapeDtypeStruct(s, d) for s, d, _ in shapes] + [VMEM((1, 128), f32)],
        in_specs=[pl.BlockSpec(memory_space=SMEM)] + [pl.BlockSpec(memory_space=VMEM)] * 9,
        out_specs=[pl.BlockSpec(memory_space=m) for _, _, m in shapes]
        + [pl.BlockSpec(memory_space=VMEM)],
        compiler_params=limit(24),
        name="finish",
    )(step, *in_vmem([squares]), *in_hbm(grads), *in_vmem(states))


def on_device(
    gradients,
    owner_table,
    step_count,
    master,
    first_code,
    first_scale,
    first_power,
    second_code,
    second_scale,
    second_power,
):
    f32, bf16 = jnp.float32, jnp.bfloat16
    devices = lax.axis_size(EVERY)
    numel = float(devices * master.size)
    table = owner_table[0]
    (grads,) = in_vmem([gradients[0]])

    leaving = pick(1, table, grads)
    from_core = [lax.ppermute(t, "core", [(0, 1), (1, 0)]) for t in leaving]
    kept = pick(0, table, grads)
    held = [[kept[k], from_core[k]] for k in range(OWN)]

    def added(k, start, stop):
        longest = held[k][0].shape[0]
        return sum(
            p[p.shape[0] - longest + start : p.shape[0] - longest + stop].astype(f32)
            for p in held[k]
        )

    def exchanged(streams, start, size):
        parts = [added(k, start, start + size).astype(bf16) for k in streams]
        return parts[0] if len(parts) == 1 else jnp.concatenate(parts)

    for k in range(OWN):
        sent = exchanged((k,), 0, 16)
        held[k].append(lax.ppermute(sent, *STEPS[k][0]))
    state = decode(
        first_scale, first_power, second_scale, second_power, master, first_code, second_code
    )
    states = [state]
    for shift in (1, 2, 3):
        states.append(lax.ppermute(state, "expert", shifted(4, shift)))
    arrived = [lax.ppermute(exchanged((k,), 16, 8), *STEPS[k][1]) for k in range(OWN)]
    for k in range(OWN):
        held[k].append(arrived[k])
    for streams in ((0, 2), (1, 3)):
        both = lax.ppermute(exchanged(streams, 24, 4), *STEPS[streams[0]][2])
        for i, k in enumerate(streams):
            held[k].append(both[4 * i : 4 * i + 4])
    last = []
    for shift in (1, 2, 3):
        sent = jnp.concatenate(
            [added(k, 28 + shift, 29 + shift).astype(bf16) for k in range(OWN)]
        )
        last.append(lax.ppermute(sent, "zh", shifted(4, shift)))
    rests = [added(k, 28, 29)[0] for k in range(OWN)]
    owned, rounded, rows = total(rests, last, devices)
    squares = lax.all_to_all(rows, EVERY, split_axis=0, concat_axis=0, tiled=True)
    sums = [owned]
    for shift in (1, 2, 3):
        sums.append(lax.ppermute(rounded, "expert", shifted(4, shift)))
    outs = finish(numel, step_count, squares.reshape(devices, -1), sums, states)
    return (*outs[:8], outs[8][0, : 4 * OWN].astype(bf16))


def solution(mesh):
    split = Mesh(
        mesh.devices.reshape(4, 4, 2, 2, mesh.shape["expert"]), EVERY
    )
    tiles = P(DP_EXPERT, None, None)
    each = P(DP_EXPERT)
    return jax.shard_map(
        on_device,
        mesh=split,
        in_specs=(
            P(DP, "expert", None, None),
            P("expert", None),
            P(),
            tiles,
            tiles,
            each,
            each,
            tiles,
            each,
            each,
        ),
        out_specs=(
            tiles,
            tiles,
            each,
            each,
            tiles,
            each,
            each,
            P(DP, None, None),
            P(DP),
        ),
        check_vma=False,
    )
```

time: 138 us -> 112 us (0.81)
  other arithmetic: 17 us -> 1.81 us
  Pallas kernels: 17.8 us -> 8.62 us
  local copies, waits for them, and re-layouts: 2.82 us -> 7.38 us
  starting transfers between devices: 63 us -> 59.6 us
  waiting for transfers between devices: 35.1 us -> 33 us
    all_to_all x1, waiting for transfers between devices: 12 us -> 1.44 us  [on_device(): lax.all_to_all(rows, EVERY, split_axis=0, concat_axis=0, tiled=True)]
    convert_element_type x13 -> x12, other arithmetic: 10.8 us -> 1.31 us  [exchanged(): parts = [added(k, start, start + size).astype(bf16) for k in streams]]
    pallas_call x3, Pallas kernels: 10.4 us -> 4.24 us  [the longest x2 3.38 us: pick(): pl.pallas_call(body, out_shape=[VMEM((count, *tile), grads.dtype)] * OWN,...]
    unnamed x20 -> x26, local copies, waits for them, and re-layouts: 1.59 us -> 6.87 us
    ppermute x18 -> x16, waiting for transfers between devices: 20.7 us -> 25.2 us  [the longest x4 9.62 us: on_device(): held[k].append(lax.ppermute(sent, *STEPS[k][0]))]
    squeeze x4 -> x2, other arithmetic: 4.14 us -> 0.09 us  [on_device(): rests = [added(k, 28, 29)[0] for k in range(OWN)]]
    ppermute x3, waiting for transfers between devices: 2.37 us -> 6.37 us  [on_device(): last.append(lax.ppermute(sent, 'zh', shifted(4, shift)))]
    convert_element_type x4, other arithmetic: 1.96 us -> 0.29 us  [on_device(): added(k, 28 + shift, 29 + shift).astype(bf16)]
  transfers between devices with their start and end apart: 26 -> 24, of which waited for: 10 -> 14; matrix products, arithmetic and copies ran while one was open for 12% -> 2% of each run, Pallas kernels for 6% -> 3%
where the time goes in v2:
time: 112 us
  starting transfers between devices  59.6 us (53%)
  waiting for transfers between devices  33 us (29%)
  Pallas kernels  8.62 us (8%)
  local copies, waits for them, and re-layouts  7.38 us (7%)
  other arithmetic  1.81 us (2%)
  between operations  1.62 us (1%)
    all_to_all x1, starting transfers between devices, on_device(): lax.all_to_all(rows, EVERY, split_axis=0, concat_axis=0, tiled=True)  17.3 us
    ppermute x4, starting transfers between devices, on_device(): held[k].append(lax.ppermute(sent, *STEPS[k][0]))  10.6 us
    ppermute x4, waiting for transfers between devices, on_device(): held[k].append(lax.ppermute(sent, *STEPS[k][0]))  9.62 us
    ppermute x4, starting transfers between devices, on_device(): lax.ppermute(exchanged((k,), 16, 8), *STEPS[k][1])  9.04 us
    unnamed x26, local copies, waits for them, and re-layouts  6.87 us
    ppermute x3, waiting for transfers between devices, on_device(): last.append(lax.ppermute(sent, 'zh', shifted(4, shift)))  6.37 us
    ppermute x3, starting transfers between devices, on_device(): last.append(lax.ppermute(sent, 'zh', shifted(4, shift)))  6.35 us
    ppermute x4, waiting for transfers between devices, on_device(): lax.ppermute(exchanged((k,), 16, 8), *STEPS[k][1])  6.33 us
  transfers between devices with their start and end apart: 24, of which 14 were waited for; matrix products, arithmetic and copies ran while one was open for 2% of the time, Pallas kernels for 3%

profile of v2, /device:TPU:1, one launch (start us, length us, event | category | flops | bytes accessed | tf_op | source)
XLA Modules:
  0.0 112.1 jit_solution(4106925611367380881)
XLA Ops:
  0.7 3.4 %copy-done = bf16[1,256,128,128]{3,2,1,0:T(8,128)(2,1)S(1)} copy-done((bf16[1,256,128,128]{3,2,1,0:T(8,128)(2,1)S(1)}, bf16[1,256,128,128]{3,2,1,0:T(8,128)(2,1)}, u32[]{:S(2)}) %copy-start) | copy-done | bytes 8388632
  4.1 0.7 copy-done.5
  4.8 1.7 %pick.3 = (bf16[32,128,128]{2,1,0:T(8,128)(2,1)S(1)}, bf16[32,128,128]{2,1,0:T(8,128)(2,1)S(1)}, bf16[32,128,128]{2,1,0:T(8,128)(2,1)S(1)}, bf16[32,128,128]{2,1,0:T(8,128)(2,1)S(1)}) custom-call(s32[256]{0:T(256)S(1)} %bitcast.16, bf16[256,128,128]{2,1,0:T(8,128)(2,1)S(1)} %bitcast.13), custom_call_target="tpu_custom_call" | custom-call | tf_op jit(solution)/shard_map/pick/pallas_call | solution.py:84
  6.5 3.3 %collective-permute-start.3 = (bf16[32,128,128]{2,1,0:T(8,128)(2,1)S(1)}, bf16[32,128,128]{2,1,0:T(8,128)(2,1)S(1)}, u32[]{:S(2)}, u32[]{:S(2)}) collective-permute-start(bf16[32,128,128]{2,1,0:T(8,128)(2,1)S(1)} %get-tuple-element.32), channel_id=1, source_target_pairs={{0,4},{4,0},{1,5},{5,1},{2,6},{6,2},{3,7},{7,3},{8,12},{12,8},{9,1... | collective-permute-start | bytes 3145736 | tf_op jit(solution)/shard_map/ppermute | solution.py:246
  9.9 0.4 collective-permute-start.7
  10.4 0.9 copy-done.2
  11.3 0.9 copy-done.3
  12.3 0.9 copy-done.4
  13.2 0.8 decode.1.refs_6_
  14.0 1.7 %pick.2 = (bf16[32,128,128]{2,1,0:T(8,128)(2,1)S(1)}, bf16[32,128,128]{2,1,0:T(8,128)(2,1)S(1)}, bf16[32,128,128]{2,1,0:T(8,128)(2,1)S(1)}, bf16[32,128,128]{2,1,0:T(8,128)(2,1)S(1)}) custom-call(s32[256]{0:T(256)S(1)} %bitcast.17, bf16[256,128,128]{2,1,0:T(8,128)(2,1)S(1)} %bitcast.14), custom_call_target="tpu_custom_call" | custom-call | tf_op jit(solution)/shard_map/pick/pallas_call | solution.py:84
  15.7 2.0 %collective-permute-start.21 = (f32[12,128,128]{2,1,0:T(8,128)S(1)}, f32[12,128,128]{2,1,0:T(8,128)S(1)}, u32[]{:S(2)}, u32[]{:S(2)}) collective-permute-start(f32[12,128,128]{2,1,0:T(8,128)S(1)} %decode.1.refs_6_), channel_id=1, source_target_pairs={{0,2},{1,3},{2,0},{3,1},{4,6},{5,7},{6,4},{7,5},{8,10},{9,11},{10,... | collective-permute-start | bytes 2359304 | tf_op jit(solution)/shard_map/ppermute | solution.py:269
  17.9 1.7 %collective-permute-start.4 = (bf16[16,128,128]{2,1,0:T(8,128)(2,1)S(1)}, bf16[16,128,128]{2,1,0:T(8,128)(2,1)S(1)}, u32[]{:S(2)}, u32[]{:S(2)}) collective-permute-start(bf16[16,128,128]{2,1,0:T(8,128)(2,1)S(1)} %add_convert_fusion.2), channel_id=1, source_target_pairs={{0,8},{8,0},{16,24},{24,16},{32,40},{40,32},{48,56},{56,48},{1,9},... | collective-permute-start | bytes 1572872 | tf_op jit(solution)/shard_map/ppermute | solution.py:263
  19.6 0.1 add_convert_fusion
  19.8 4.8 %collective-permute-start.11 = (bf16[16,128,128]{2,1,0:T(8,128)(2,1)S(1)}, bf16[16,128,128]{2,1,0:T(8,128)(2,1)S(1)}, u32[]{:S(2)}, u32[]{:S(2)}) collective-permute-start(bf16[16,128,128]{2,1,0:T(8,128)(2,1)S(1)} %add_convert_fusion), channel_id=1, source_target_pairs={{0,56},{8,16},{16,8},{24,32},{32,24},{40,48},{48,40},{56,0},{1,57}... | collective-permute-start | bytes 1572872 | tf_op jit(solution)/shard_map/ppermute | solution.py:263
  24.6 0.1 add_convert_fusion.1
  24.7 2.8 %collective-permute-start.8 = (bf16[16,128,128]{2,1,0:T(8,128)(2,1)S(1)}, bf16[16,128,128]{2,1,0:T(8,128)(2,1)S(1)}, u32[]{:S(2)}, u32[]{:S(2)}) collective-permute-start(bf16[16,128,128]{2,1,0:T(8,128)(2,1)S(1)} %add_convert_fusion.1), channel_id=1, source_target_pairs={{0,192},{64,128},{128,64},{192,0},{1,193},{65,129},{129,65},{193,1... | collective-permute-start | bytes 1572872 | tf_op jit(solution)/shard_map/ppermute | solution.py:263
  27.5 0.1 add_convert_fusion.3
  27.7 3.2 %collective-permute-done.4 = bf16[16,128,128]{2,1,0:T(8,128)(2,1)S(1)} collective-permute-done((bf16[16,128,128]{2,1,0:T(8,128)(2,1)S(1)}, bf16[16,128,128]{2,1,0:T(8,128)(2,1)S(1)}, u32[]{:S(2)}, u32[]{:S(2)}) %collective-permute-start.4) | collective-permute-done | bytes 524320 | tf_op jit(solution)/shard_map/ppermute | solution.py:263
  30.9 1.3 %collective-permute-start.1 = (bf16[16,128,128]{2,1,0:T(8,128)(2,1)S(1)}, bf16[16,128,128]{2,1,0:T(8,128)(2,1)S(1)}, u32[]{:S(2)}, u32[]{:S(2)}) collective-permute-start(bf16[16,128,128]{2,1,0:T(8,128)(2,1)S(1)} %add_convert_fusion.3), channel_id=1, source_target_pairs={{0,64},{64,0},{128,192},{192,128},{1,65},{65,1},{129,193},{193,129... | collective-permute-start | bytes 1572872 | tf_op jit(solution)/shard_map/ppermute | solution.py:263
  32.3 3.3 %collective-permute-done.11 = bf16[16,128,128]{2,1,0:T(8,128)(2,1)S(1)} collective-permute-done((bf16[16,128,128]{2,1,0:T(8,128)(2,1)S(1)}, bf16[16,128,128]{2,1,0:T(8,128)(2,1)S(1)}, u32[]{:S(2)}, u32[]{:S(2)}) %collective-permute-start.11) | collective-permute-done | bytes 524320 | tf_op jit(solution)/shard_map/ppermute | solution.py:263
  35.6 1.2 %collective-permute-start.22 = (f32[12,128,128]{2,1,0:T(8,128)S(1)}, f32[12,128,128]{2,1,0:T(8,128)S(1)}, u32[]{:S(2)}, u32[]{:S(2)}) collective-permute-start(f32[12,128,128]{2,1,0:T(8,128)S(1)} %decode.1.refs_6_), channel_id=1, source_target_pairs={{0,3},{1,0},{2,1},{3,2},{4,7},{5,4},{6,5},{7,6},{8,11},{9,8},{10,9... | collective-permute-start | bytes 2359304 | tf_op jit(solution)/shard_map/ppermute | solution.py:269
  36.9 1.2 %collective-permute-done.8 = bf16[16,128,128]{2,1,0:T(8,128)(2,1)S(1)} collective-permute-done((bf16[16,128,128]{2,1,0:T(8,128)(2,1)S(1)}, bf16[16,128,128]{2,1,0:T(8,128)(2,1)S(1)}, u32[]{:S(2)}, u32[]{:S(2)}) %collective-permute-start.8) | collective-permute-done | bytes 524320 | tf_op jit(solution)/shard_map/ppermute | solution.py:263
  38.1 2.6 %collective-permute-start.12 = (bf16[8,128,128]{2,1,0:T(8,128)(2,1)S(1)}, bf16[8,128,128]{2,1,0:T(8,128)(2,1)S(1)}, u32[]{:S(2)}, u32[]{:S(2)}) collective-permute-start(bf16[8,128,128]{2,1,0:T(8,128)(2,1)S(1)} %add_convert_fusion.4), channel_id=1, source_target_pairs={{0,192},{64,128},{128,64},{192,0},{1,193},{65,129},{129,65},{193,1... | collective-permute-start | bytes 786440 | tf_op jit(solution)/shard_map/ppermute | solution.py:270
  40.8 1.9 %collective-permute-done.1 = bf16[16,128,128]{2,1,0:T(8,128)(2,1)S(1)} collective-permute-done((bf16[16,128,128]{2,1,0:T(8,128)(2,1)S(1)}, bf16[16,128,128]{2,1,0:T(8,128)(2,1)S(1)}, u32[]{:S(2)}, u32[]{:S(2)}) %collective-permute-start.1) | collective-permute-done | bytes 524320 | tf_op jit(solution)/shard_map/ppermute | solution.py:263
  42.7 5.0 %collective-permute-start.9 = (bf16[8,128,128]{2,1,0:T(8,128)(2,1)S(1)}, bf16[8,128,128]{2,1,0:T(8,128)(2,1)S(1)}, u32[]{:S(2)}, u32[]{:S(2)}) collective-permute-start(bf16[8,128,128]{2,1,0:T(8,128)(2,1)S(1)} %add_convert_fusion.5), channel_id=1, source_target_pairs={{0,56},{8,16},{16,8},{24,32},{32,24},{40,48},{48,40},{56,0},{1,57}... | collective-permute-start | bytes 786440 | tf_op jit(solution)/shard_map/ppermute | solution.py:270
  47.9 1.4 %collective-permute-start.5 = (bf16[8,128,128]{2,1,0:T(8,128)(2,1)S(1)}, bf16[8,128,128]{2,1,0:T(8,128)(2,1)S(1)}, u32[]{:S(2)}, u32[]{:S(2)}) collective-permute-start(bf16[8,128,128]{2,1,0:T(8,128)(2,1)S(1)} %add_convert_fusion.6), channel_id=1, source_target_pairs={{0,64},{64,0},{128,192},{192,128},{1,65},{65,1},{129,193},{193,129... | collective-permute-start | bytes 786440 | tf_op jit(solution)/shard_map/ppermute | solution.py:270
  49.3 2.3 %collective-permute-done.9 = bf16[8,128,128]{2,1,0:T(8,128)(2,1)S(1)} collective-permute-done((bf16[8,128,128]{2,1,0:T(8,128)(2,1)S(1)}, bf16[8,128,128]{2,1,0:T(8,128)(2,1)S(1)}, u32[]{:S(2)}, u32[]{:S(2)}) %collective-permute-start.9) | collective-permute-done | bytes 262176 | tf_op jit(solution)/shard_map/ppermute | solution.py:270
  51.7 1.7 %collective-permute-done.5 = bf16[8,128,128]{2,1,0:T(8,128)(2,1)S(1)} collective-permute-done((bf16[8,128,128]{2,1,0:T(8,128)(2,1)S(1)}, bf16[8,128,128]{2,1,0:T(8,128)(2,1)S(1)}, u32[]{:S(2)}, u32[]{:S(2)}) %collective-permute-start.5) | collective-permute-done | bytes 262176 | tf_op jit(solution)/shard_map/ppermute | solution.py:270
  53.5 1.3 %collective-permute-start.13 = (bf16[8,128,128]{2,1,0:T(8,128)(2,1)S(1)}, bf16[8,128,128]{2,1,0:T(8,128)(2,1)S(1)}, u32[]{:S(2)}, u32[]{:S(2)}) collective-permute-start(bf16[8,128,128]{2,1,0:T(8,128)(2,1)S(1)} %pad_maximum_fusion.1), channel_id=1, source_target_pairs={{0,64},{64,0},{128,192},{192,128},{1,65},{65,1},{129,193},{193,129... | collective-permute-start | bytes 786440 | tf_op jit(solution)/shard_map/ppermute | solution.py:274
  54.8 2.3 %collective-permute-done.2 = bf16[8,128,128]{2,1,0:T(8,128)(2,1)S(1)} collective-permute-done((bf16[8,128,128]{2,1,0:T(8,128)(2,1)S(1)}, bf16[8,128,128]{2,1,0:T(8,128)(2,1)S(1)}, u32[]{:S(2)}, u32[]{:S(2)}) %collective-permute-start.2) | collective-permute-done | bytes 262176 | tf_op jit(solution)/shard_map/ppermute | solution.py:270
  57.3 2.9 %collective-permute-start.6 = (bf16[8,128,128]{2,1,0:T(8,128)(2,1)S(1)}, bf16[8,128,128]{2,1,0:T(8,128)(2,1)S(1)}, u32[]{:S(2)}, u32[]{:S(2)}) collective-permute-start(bf16[8,128,128]{2,1,0:T(8,128)(2,1)S(1)} %pad_maximum_fusion), channel_id=1, source_target_pairs={{0,192},{64,128},{128,64},{192,0},{1,193},{65,129},{129,65},{193,1... | collective-permute-start | bytes 786440 | tf_op jit(solution)/shard_map/ppermute | solution.py:274
  60.3 3.7 %collective-permute-done.6 = bf16[8,128,128]{2,1,0:T(8,128)(2,1)S(1)} collective-permute-done((bf16[8,128,128]{2,1,0:T(8,128)(2,1)S(1)}, bf16[8,128,128]{2,1,0:T(8,128)(2,1)S(1)}, u32[]{:S(2)}, u32[]{:S(2)}) %collective-permute-start.6) | collective-permute-done | bytes 262176 | tf_op jit(solution)/shard_map/ppermute | solution.py:274
  64.1 0.5 collective-permute-start.14
  64.6 4.1 %collective-permute-start.15 = (bf16[4,128,128]{2,1,0:T(8,128)(2,1)S(1)}, bf16[4,128,128]{2,1,0:T(8,128)(2,1)S(1)}, u32[]{:S(2)}, u32[]{:S(2)}) collective-permute-start(bf16[4,128,128]{2,1,0:T(8,128)(2,1)S(1)} %pad_maximum_fusion.3), channel_id=1, source_target_pairs={{0,32},{16,48},{32,0},{48,16},{1,33},{17,49},{33,1},{49,17},{2,34}... | collective-permute-start | bytes 393224 | tf_op jit(solution)/shard_map/ppermute | solution.py:282
  68.8 1.4 %collective-permute-done.14.refs_4_ = bf16[4,128,128]{2,1,0:T(8,128)(2,1)S(1)} collective-permute-done((bf16[4,128,128]{2,1,0:T(8,128)(2,1)S(1)}, bf16[4,128,128]{2,1,0:T(8,128)(2,1)S(1)}, u32[]{:S(2)}, u32[]{:S(2)}) %collective-permute-start.14) | collective-permute-done | bytes 131104 | tf_op jit(solution)/shard_map/ppermute | solution.py:282
  70.3 1.8 %collective-permute-start.16 = (bf16[4,128,128]{2,1,0:T(8,128)(2,1)S(1)}, bf16[4,128,128]{2,1,0:T(8,128)(2,1)S(1)}, u32[]{:S(2)}, u32[]{:S(2)}) collective-permute-start(bf16[4,128,128]{2,1,0:T(8,128)(2,1)S(1)} %pad_maximum_fusion.4), channel_id=1, source_target_pairs={{0,48},{16,0},{32,16},{48,32},{1,49},{17,1},{33,17},{49,33},{2,50}... | collective-permute-start | bytes 393224 | tf_op jit(solution)/shard_map/ppermute | solution.py:282
  72.1 1.9 %collective-permute-done.15.refs_5_ = bf16[4,128,128]{2,1,0:T(8,128)(2,1)S(1)} collective-permute-done((bf16[4,128,128]{2,1,0:T(8,128)(2,1)S(1)}, bf16[4,128,128]{2,1,0:T(8,128)(2,1)S(1)}, u32[]{:S(2)}, u32[]{:S(2)}) %collective-permute-start.15) | collective-permute-done | bytes 131104 | tf_op jit(solution)/shard_map/ppermute | solution.py:282
  74.0 3.1 %collective-permute-done.16.refs_6_ = bf16[4,128,128]{2,1,0:T(8,128)(2,1)S(1)} collective-permute-done((bf16[4,128,128]{2,1,0:T(8,128)(2,1)S(1)}, bf16[4,128,128]{2,1,0:T(8,128)(2,1)S(1)}, u32[]{:S(2)}, u32[]{:S(2)}) %collective-permute-start.16) | collective-permute-done | bytes 131104 | tf_op jit(solution)/shard_map/ppermute | solution.py:282
  77.0 0.9 total.1
  77.9 17.3 %all-to-all-start = ((f32[256,1,128]{2,1,0:T(1,128)}), f32[256,1,128]{2,1,0:T(1,128)S(1)}, u32[]{:S(2)}, u32[]{:S(2)}) async-start(f32[256,1,128]{2,1,0:T(1,128)} %get-tuple-element.37), calls=%async_computation | async-start | bytes 262144 | tf_op jit(solution)/shard_map/all_to_all | solution.py:285
  95.2 1.4 %collective-permute-start.17 = (bf16[4,128,128]{2,1,0:T(8,128)(2,1)}, bf16[4,128,128]{2,1,0:T(8,128)(2,1)S(1)}, u32[]{:S(2)}, u32[]{:S(2)}) collective-permute-start(bf16[4,128,128]{2,1,0:T(8,128)(2,1)} %get-tuple-element.39), channel_id=1, source_target_pairs={{0,1},{1,2},{2,3},{3,0},{4,5},{5,6},{6,7},{7,4},{8,9},{9,10},{10,1... | collective-permute-start | bytes 393224 | tf_op jit(solution)/shard_map/ppermute | solution.py:288
  96.6 2.4 %collective-permute-start.18 = (bf16[4,128,128]{2,1,0:T(8,128)(2,1)}, bf16[4,128,128]{2,1,0:T(8,128)(2,1)S(1)}, u32[]{:S(2)}, u32[]{:S(2)}) collective-permute-start(bf16[4,128,128]{2,1,0:T(8,128)(2,1)} %get-tuple-element.39), channel_id=1, source_target_pairs={{0,2},{1,3},{2,0},{3,1},{4,6},{5,7},{6,4},{7,5},{8,10},{9,11},{10,... | collective-permute-start | bytes 393224 | tf_op jit(solution)/shard_map/ppermute | solution.py:288
  99.0 1.2 %collective-permute-start.19 = (bf16[4,128,128]{2,1,0:T(8,128)(2,1)}, bf16[4,128,128]{2,1,0:T(8,128)(2,1)}, u32[]{:S(2)}, u32[]{:S(2)}) collective-permute-start(bf16[4,128,128]{2,1,0:T(8,128)(2,1)} %get-tuple-element.39), channel_id=1, source_target_pairs={{0,3},{1,0},{2,1},{3,2},{4,7},{5,4},{6,5},{7,6},{8,11},{9,8},{10,9... | collective-permute-start | bytes 393224 | tf_op jit(solution)/shard_map/ppermute | solution.py:288
  100.9 0.2 collective-permute-done.17.refs_3_
  101.1 5.4 %collective-permute-done.18.refs_4_ = bf16[4,128,128]{2,1,0:T(8,128)(2,1)S(1)} collective-permute-done((bf16[4,128,128]{2,1,0:T(8,128)(2,1)}, bf16[4,128,128]{2,1,0:T(8,128)(2,1)S(1)}, u32[]{:S(2)}, u32[]{:S(2)}) %collective-permute-start.18) | collective-permute-done | bytes 131104 | tf_op jit(solution)/shard_map/ppermute | solution.py:288
  106.5 1.4 %all-to-all-done = f32[256,1,128]{2,1,0:T(1,128)S(1)} async-done(((f32[256,1,128]{2,1,0:T(1,128)}), f32[256,1,128]{2,1,0:T(1,128)S(1)}, u32[]{:S(2)}, u32[]{:S(2)}) %all-to-all-start) | async-done | bytes 131104 | tf_op jit(solution)/shard_map/all_to_all | solution.py:285
  107.9 3.6 %finish.1 = (f32[4,128,128]{2,1,0:T(8,128)}, bf16[4,128,128]{2,1,0:T(8,128)(2,1)}, f32[4]{0:T(128)}, f32[4]{0:T(128)}, bf16[4,128,128]{2,1,0:T(8,128)(2,1)}, /*i...) custom-call(s32[1]{0:T(128)S(6)} %copy.20.refs_0_, f32[256,128]{1,0:T(8,128)S(1)} %bitcast.15, ...), custom_call_target="tpu_custom_call" | custom-call | tf_op jit(solution)/shard_map/finish/pallas_call | solution.py:216
  111.6 0.5 slice_bitcast_fusion
  (56 shorter events, 1.7 us)
Async XLA Ops:
  0.6 13.4 %copy-start.6 = (s32[1,256]{1,0:T(1,128)S(1)}, s32[1,256]{1,0:T(1,128)}, u32[]{:S(2)}) copy-start(s32[1,256]{1,0:T(1,128)} %param.11) | copy-start | bytes 3076
  0.7 9.7 %copy-start.7 = (f32[4]{0:T(128)S(1)}, f32[4]{0:T(128)}, u32[]{:S(2)}) copy-start(f32[4]{0:T(128)} %fs.1) | copy-start | bytes 52
  0.7 9.7 %copy-start.8 = (f32[4]{0:T(128)S(1)}, f32[4]{0:T(128)}, u32[]{:S(2)}) copy-start(f32[4]{0:T(128)} %fp.1) | copy-start | bytes 52
  0.7 9.7 %copy-start.9 = (f32[4]{0:T(128)S(1)}, f32[4]{0:T(128)}, u32[]{:S(2)}) copy-start(f32[4]{0:T(128)} %ss.1) | copy-start | bytes 52
  0.7 9.7 %copy-start.10 = (f32[4]{0:T(128)S(1)}, f32[4]{0:T(128)}, u32[]{:S(2)}) copy-start(f32[4]{0:T(128)} %sp.1) | copy-start | bytes 52
  0.7 3.4 %copy-start = (bf16[1,256,128,128]{3,2,1,0:T(8,128)(2,1)S(1)}, bf16[1,256,128,128]{3,2,1,0:T(8,128)(2,1)}, u32[]{:S(2)}) copy-start(bf16[1,256,128,128]{3,2,1,0:T(8,128)(2,1)} %param.10) | copy-start | bytes 25165828
  4.1 0.7 copy-start.5
  4.8 9.2 %copy-start.1 = (bf16[1,256,128,128]{3,2,1,0:T(8,128)(2,1)S(1)}, bf16[1,256,128,128]{3,2,1,0:T(8,128)(2,1)}, u32[]{:S(2)}) copy-start(bf16[1,256,128,128]{3,2,1,0:T(8,128)(2,1)} %param.10) | copy-start | bytes 25165828
  6.5 9.3 %collective-permute-start.3 = (bf16[32,128,128]{2,1,0:T(8,128)(2,1)S(1)}, bf16[32,128,128]{2,1,0:T(8,128)(2,1)S(1)}, u32[]{:S(2)}, u32[]{:S(2)}) collective-permute-start(bf16[32,128,128]{2,1,0:T(8,128)(2,1)S(1)} %get-tuple-element.32), channel_id=1, source_target_pairs={{0,4},{4,0},{1,5},{5,1},{2,6},{6,2},{3,7},{7,3},{8,12},{12,8},{9,1... | collective-permute-start | bytes 3145736 | tf_op jit(solution)/shard_map/ppermute | solution.py:246
  9.8 8.1 %collective-permute-start.10 = (bf16[32,128,128]{2,1,0:T(8,128)(2,1)S(1)}, bf16[32,128,128]{2,1,0:T(8,128)(2,1)S(1)}, u32[]{:S(2)}, u32[]{:S(2)}) collective-permute-start(bf16[32,128,128]{2,1,0:T(8,128)(2,1)S(1)} %get-tuple-element.36), channel_id=1, source_target_pairs={{0,4},{4,0},{1,5},{5,1},{2,6},{6,2},{3,7},{7,3},{8,12},{12,8},{9,1... | collective-permute-start | bytes 3145736 | tf_op jit(solution)/shard_map/ppermute | solution.py:246
  9.9 9.9 %collective-permute-start.7 = (bf16[32,128,128]{2,1,0:T(8,128)(2,1)S(1)}, bf16[32,128,128]{2,1,0:T(8,128)(2,1)S(1)}, u32[]{:S(2)}, u32[]{:S(2)}) collective-permute-start(bf16[32,128,128]{2,1,0:T(8,128)(2,1)S(1)} %get-tuple-element.34), channel_id=1, source_target_pairs={{0,4},{4,0},{1,5},{5,1},{2,6},{6,2},{3,7},{7,3},{8,12},{12,8},{9,1... | collective-permute-start | bytes 3145736 | tf_op jit(solution)/shard_map/ppermute | solution.py:246
  10.3 14.4 %collective-permute-start = (bf16[32,128,128]{2,1,0:T(8,128)(2,1)S(1)}, bf16[32,128,128]{2,1,0:T(8,128)(2,1)S(1)}, u32[]{:S(2)}, u32[]{:S(2)}) collective-permute-start(bf16[32,128,128]{2,1,0:T(8,128)(2,1)S(1)} %get-tuple-element.30), channel_id=1, source_target_pairs={{0,4},{4,0},{1,5},{5,1},{2,6},{6,2},{3,7},{7,3},{8,12},{12,8},{9,1... | collective-permute-start | bytes 3145736 | tf_op jit(solution)/shard_map/ppermute | solution.py:246
  10.4 1.0 copy-start.2
  11.3 0.9 copy-start.3
  12.3 0.9 copy-start.4
  13.9 85.1 %collective-permute-start.20 = (f32[12,128,128]{2,1,0:T(8,128)S(1)}, f32[12,128,128]{2,1,0:T(8,128)S(1)}, u32[]{:S(2)}, u32[]{:S(2)}) collective-permute-start(f32[12,128,128]{2,1,0:T(8,128)S(1)} %decode.1.refs_6_), channel_id=1, source_target_pairs={{0,1},{1,2},{2,3},{3,0},{4,5},{5,6},{6,7},{7,4},{8,9},{9,10},{10,1... | collective-permute-start | bytes 2359304 | tf_op jit(solution)/shard_map/ppermute | solution.py:269
  15.7 85.1 %collective-permute-start.21 = (f32[12,128,128]{2,1,0:T(8,128)S(1)}, f32[12,128,128]{2,1,0:T(8,128)S(1)}, u32[]{:S(2)}, u32[]{:S(2)}) collective-permute-start(f32[12,128,128]{2,1,0:T(8,128)S(1)} %decode.1.refs_6_), channel_id=1, source_target_pairs={{0,2},{1,3},{2,0},{3,1},{4,6},{5,7},{6,4},{7,5},{8,10},{9,11},{10,... | collective-permute-start | bytes 2359304 | tf_op jit(solution)/shard_map/ppermute | solution.py:269
  17.9 13.0 %collective-permute-start.4 = (bf16[16,128,128]{2,1,0:T(8,128)(2,1)S(1)}, bf16[16,128,128]{2,1,0:T(8,128)(2,1)S(1)}, u32[]{:S(2)}, u32[]{:S(2)}) collective-permute-start(bf16[16,128,128]{2,1,0:T(8,128)(2,1)S(1)} %add_convert_fusion.2), channel_id=1, source_target_pairs={{0,8},{8,0},{16,24},{24,16},{32,40},{40,32},{48,56},{56,48},{1,9},... | collective-permute-start | bytes 1572872 | tf_op jit(solution)/shard_map/ppermute | solution.py:263
  19.8 15.8 %collective-permute-start.11 = (bf16[16,128,128]{2,1,0:T(8,128)(2,1)S(1)}, bf16[16,128,128]{2,1,0:T(8,128)(2,1)S(1)}, u32[]{:S(2)}, u32[]{:S(2)}) collective-permute-start(bf16[16,128,128]{2,1,0:T(8,128)(2,1)S(1)} %add_convert_fusion), channel_id=1, source_target_pairs={{0,56},{8,16},{16,8},{24,32},{32,24},{40,48},{48,40},{56,0},{1,57}... | collective-permute-start | bytes 1572872 | tf_op jit(solution)/shard_map/ppermute | solution.py:263
  24.7 13.4 %collective-permute-start.8 = (bf16[16,128,128]{2,1,0:T(8,128)(2,1)S(1)}, bf16[16,128,128]{2,1,0:T(8,128)(2,1)S(1)}, u32[]{:S(2)}, u32[]{:S(2)}) collective-permute-start(bf16[16,128,128]{2,1,0:T(8,128)(2,1)S(1)} %add_convert_fusion.1), channel_id=1, source_target_pairs={{0,192},{64,128},{128,64},{192,0},{1,193},{65,129},{129,65},{193,1... | collective-permute-start | bytes 1572872 | tf_op jit(solution)/shard_map/ppermute | solution.py:263
  30.9 11.8 %collective-permute-start.1 = (bf16[16,128,128]{2,1,0:T(8,128)(2,1)S(1)}, bf16[16,128,128]{2,1,0:T(8,128)(2,1)S(1)}, u32[]{:S(2)}, u32[]{:S(2)}) collective-permute-start(bf16[16,128,128]{2,1,0:T(8,128)(2,1)S(1)} %add_convert_fusion.3), channel_id=1, source_target_pairs={{0,64},{64,0},{128,192},{192,128},{1,65},{65,1},{129,193},{193,129... | collective-permute-start | bytes 1572872 | tf_op jit(solution)/shard_map/ppermute | solution.py:263
  35.6 65.3 %collective-permute-start.22 = (f32[12,128,128]{2,1,0:T(8,128)S(1)}, f32[12,128,128]{2,1,0:T(8,128)S(1)}, u32[]{:S(2)}, u32[]{:S(2)}) collective-permute-start(f32[12,128,128]{2,1,0:T(8,128)S(1)} %decode.1.refs_6_), channel_id=1, source_target_pairs={{0,3},{1,0},{2,1},{3,2},{4,7},{5,4},{6,5},{7,6},{8,11},{9,8},{10,9... | collective-permute-start | bytes 2359304 | tf_op jit(solution)/shard_map/ppermute | solution.py:269
  38.1 9.8 %collective-permute-start.12 = (bf16[8,128,128]{2,1,0:T(8,128)(2,1)S(1)}, bf16[8,128,128]{2,1,0:T(8,128)(2,1)S(1)}, u32[]{:S(2)}, u32[]{:S(2)}) collective-permute-start(bf16[8,128,128]{2,1,0:T(8,128)(2,1)S(1)} %add_convert_fusion.4), channel_id=1, source_target_pairs={{0,192},{64,128},{128,64},{192,0},{1,193},{65,129},{129,65},{193,1... | collective-permute-start | bytes 786440 | tf_op jit(solution)/shard_map/ppermute | solution.py:270
  42.7 8.9 %collective-permute-start.9 = (bf16[8,128,128]{2,1,0:T(8,128)(2,1)S(1)}, bf16[8,128,128]{2,1,0:T(8,128)(2,1)S(1)}, u32[]{:S(2)}, u32[]{:S(2)}) collective-permute-start(bf16[8,128,128]{2,1,0:T(8,128)(2,1)S(1)} %add_convert_fusion.5), channel_id=1, source_target_pairs={{0,56},{8,16},{16,8},{24,32},{32,24},{40,48},{48,40},{56,0},{1,57}... | collective-permute-start | bytes 786440 | tf_op jit(solution)/shard_map/ppermute | solution.py:270
  47.9 5.6 %collective-permute-start.5 = (bf16[8,128,128]{2,1,0:T(8,128)(2,1)S(1)}, bf16[8,128,128]{2,1,0:T(8,128)(2,1)S(1)}, u32[]{:S(2)}, u32[]{:S(2)}) collective-permute-start(bf16[8,128,128]{2,1,0:T(8,128)(2,1)S(1)} %add_convert_fusion.6), channel_id=1, source_target_pairs={{0,64},{64,0},{128,192},{192,128},{1,65},{65,1},{129,193},{193,129... | collective-permute-start | bytes 786440 | tf_op jit(solution)/shard_map/ppermute | solution.py:270
  51.6 5.5 %collective-permute-start.2 = (bf16[8,128,128]{2,1,0:T(8,128)(2,1)S(1)}, bf16[8,128,128]{2,1,0:T(8,128)(2,1)S(1)}, u32[]{:S(2)}, u32[]{:S(2)}) collective-permute-start(bf16[8,128,128]{2,1,0:T(8,128)(2,1)S(1)} %add_convert_fusion.7), channel_id=1, source_target_pairs={{0,8},{8,0},{16,24},{24,16},{32,40},{40,32},{48,56},{56,48},{1,9},... | collective-permute-start | bytes 786440 | tf_op jit(solution)/shard_map/ppermute | solution.py:270
  53.5 6.7 %collective-permute-start.13 = (bf16[8,128,128]{2,1,0:T(8,128)(2,1)S(1)}, bf16[8,128,128]{2,1,0:T(8,128)(2,1)S(1)}, u32[]{:S(2)}, u32[]{:S(2)}) collective-permute-start(bf16[8,128,128]{2,1,0:T(8,128)(2,1)S(1)} %pad_maximum_fusion.1), channel_id=1, source_target_pairs={{0,64},{64,0},{128,192},{192,128},{1,65},{65,1},{129,193},{193,129... | collective-permute-start | bytes 786440 | tf_op jit(solution)/shard_map/ppermute | solution.py:274
  57.3 6.7 %collective-permute-start.6 = (bf16[8,128,128]{2,1,0:T(8,128)(2,1)S(1)}, bf16[8,128,128]{2,1,0:T(8,128)(2,1)S(1)}, u32[]{:S(2)}, u32[]{:S(2)}) collective-permute-start(bf16[8,128,128]{2,1,0:T(8,128)(2,1)S(1)} %pad_maximum_fusion), channel_id=1, source_target_pairs={{0,192},{64,128},{128,64},{192,0},{1,193},{65,129},{129,65},{193,1... | collective-permute-start | bytes 786440 | tf_op jit(solution)/shard_map/ppermute | solution.py:274
  64.1 6.1 %collective-permute-start.14 = (bf16[4,128,128]{2,1,0:T(8,128)(2,1)S(1)}, bf16[4,128,128]{2,1,0:T(8,128)(2,1)S(1)}, u32[]{:S(2)}, u32[]{:S(2)}) collective-permute-start(bf16[4,128,128]{2,1,0:T(8,128)(2,1)S(1)} %pad_maximum_fusion.2), channel_id=1, source_target_pairs={{0,16},{16,32},{32,48},{48,0},{1,17},{17,33},{33,49},{49,1},{2,18}... | collective-permute-start | bytes 393224 | tf_op jit(solution)/shard_map/ppermute | solution.py:282
  64.6 9.3 %collective-permute-start.15 = (bf16[4,128,128]{2,1,0:T(8,128)(2,1)S(1)}, bf16[4,128,128]{2,1,0:T(8,128)(2,1)S(1)}, u32[]{:S(2)}, u32[]{:S(2)}) collective-permute-start(bf16[4,128,128]{2,1,0:T(8,128)(2,1)S(1)} %pad_maximum_fusion.3), channel_id=1, source_target_pairs={{0,32},{16,48},{32,0},{48,16},{1,33},{17,49},{33,1},{49,17},{2,34}... | collective-permute-start | bytes 393224 | tf_op jit(solution)/shard_map/ppermute | solution.py:282
  70.3 6.8 %collective-permute-start.16 = (bf16[4,128,128]{2,1,0:T(8,128)(2,1)S(1)}, bf16[4,128,128]{2,1,0:T(8,128)(2,1)S(1)}, u32[]{:S(2)}, u32[]{:S(2)}) collective-permute-start(bf16[4,128,128]{2,1,0:T(8,128)(2,1)S(1)} %pad_maximum_fusion.4), channel_id=1, source_target_pairs={{0,48},{16,0},{32,16},{48,32},{1,49},{17,1},{33,17},{49,33},{2,50}... | collective-permute-start | bytes 393224 | tf_op jit(solution)/shard_map/ppermute | solution.py:282
  77.9 30.0 %all-to-all-start = ((f32[256,1,128]{2,1,0:T(1,128)}), f32[256,1,128]{2,1,0:T(1,128)S(1)}, u32[]{:S(2)}, u32[]{:S(2)}) async-start(f32[256,1,128]{2,1,0:T(1,128)} %get-tuple-element.37), calls=%async_computation | async-start | bytes 262144 | tf_op jit(solution)/shard_map/all_to_all | solution.py:285
  95.2 5.9 %collective-permute-start.17 = (bf16[4,128,128]{2,1,0:T(8,128)(2,1)}, bf16[4,128,128]{2,1,0:T(8,128)(2,1)S(1)}, u32[]{:S(2)}, u32[]{:S(2)}) collective-permute-start(bf16[4,128,128]{2,1,0:T(8,128)(2,1)} %get-tuple-element.39), channel_id=1, source_target_pairs={{0,1},{1,2},{2,3},{3,0},{4,5},{5,6},{6,7},{7,4},{8,9},{9,10},{10,1... | collective-permute-start | bytes 393224 | tf_op jit(solution)/shard_map/ppermute | solution.py:288
  96.6 9.8 %collective-permute-start.18 = (bf16[4,128,128]{2,1,0:T(8,128)(2,1)}, bf16[4,128,128]{2,1,0:T(8,128)(2,1)S(1)}, u32[]{:S(2)}, u32[]{:S(2)}) collective-permute-start(bf16[4,128,128]{2,1,0:T(8,128)(2,1)} %get-tuple-element.39), channel_id=1, source_target_pairs={{0,2},{1,3},{2,0},{3,1},{4,6},{5,7},{6,4},{7,5},{8,10},{9,11},{10,... | collective-permute-start | bytes 393224 | tf_op jit(solution)/shard_map/ppermute | solution.py:288
  99.0 7.4 %collective-permute-start.19 = (bf16[4,128,128]{2,1,0:T(8,128)(2,1)}, bf16[4,128,128]{2,1,0:T(8,128)(2,1)}, u32[]{:S(2)}, u32[]{:S(2)}) collective-permute-start(bf16[4,128,128]{2,1,0:T(8,128)(2,1)} %get-tuple-element.39), channel_id=1, source_target_pairs={{0,3},{1,0},{2,1},{3,2},{4,7},{5,4},{6,5},{7,6},{8,11},{9,8},{10,9... | collective-permute-start | bytes 393224 | tf_op jit(solution)/shard_map/ppermute | solution.py:288
  101.1 6.8 %copy-start.11 = (bf16[4,128,128]{2,1,0:T(8,128)(2,1)}, bf16[4,128,128]{2,1,0:T(8,128)(2,1)S(1)}, u32[]{:S(2)}) copy-start(bf16[4,128,128]{2,1,0:T(8,128)(2,1)S(1)} %collective-permute-done.17.refs_3_) | copy-start | bytes 393220
  106.5 1.5 %copy-start.12 = (bf16[4,128,128]{2,1,0:T(8,128)(2,1)}, bf16[4,128,128]{2,1,0:T(8,128)(2,1)S(1)}, u32[]{:S(2)}) copy-start(bf16[4,128,128]{2,1,0:T(8,128)(2,1)S(1)} %collective-permute-done.18.refs_4_) | copy-start | bytes 393220
